TPU v7x, 32 devices: a whole 2x2x4 slice. The times are simulated.
32 devices in a mesh: wide: 8 (over y, x, core), head: 4 (over z).
Axes of the slice: x: 2, y: 2, z: 4, core: 2. Of those that a mesh axis runs over, the one named last changes fastest.
Arguments:
- tokens: bfloat16 [16384, 1024], P(('wide', 'head')), may hold values from -6 to 6
- cotangent: bfloat16 [16384, 1024], P(('wide', 'head')), may hold values from -6 to 6
- w_query: bfloat16 [1024, 1024], P('wide', 'head'), may hold values from -0.25 to 0.25
- w_key: bfloat16 [1024, 1024], P('wide', 'head'), may hold values from -0.25 to 0.25
- w_value: bfloat16 [1024, 1024], P('wide', 'head'), may hold values from -0.1875 to 0.1875
- w_out: bfloat16 [1024, 1024], P('head', 'wide'), may hold values from -0.1875 to 0.1875
- w_up: bfloat16 [1024, 4096], P('wide', 'head'), may hold values from -0.1875 to 0.1875
- w_down: bfloat16 [4096, 1024], P('head', 'wide'), may hold values from -0.09375 to 0.09375
- norm_gain: float32 [4, 1024], replicated, may hold values from 0.25 to 1.75
- norm_bias: float32 [4, 1024], replicated, may hold values from -3 to 3
Outputs:
- block_out: bfloat16 [16384, 1024], P(('wide', 'head'))
- input_grad: float32 [16384, 1024], P(('wide', 'head'))
- grad_query: float32 [1024, 1024], P('wide', 'head')
- grad_key: float32 [1024, 1024], P('wide', 'head')
- grad_value: float32 [1024, 1024], P('wide', 'head')
- grad_out: float32 [1024, 1024], P('head', 'wide')
- grad_up: float32 [1024, 4096], P('wide', 'head')
- grad_down: float32 [4096, 1024], P('head', 'wide')
- gain_grad: float32 [4, 1024], replicated
- bias_grad: float32 [4, 1024], replicated
All inputs are finite; a program needn't handle non-finite values.
Results may differ from a plain program's by a relative error of at most 0.015.
Values may be sent and summed in bfloat16 or wider, within the bound.
No kernel may reach another device: no remote copies, remote signals or barrier semaphores. Data moves between devices by JAX's collectives and lax.ppermute only.
A program may use at most 192 MiB of HBM per device.

v0:
```python
import math

import jax
import jax.numpy as jnp
from jax import lax
from jax.sharding import PartitionSpec as P

HD = 64


EPS = 1e-05


def normalize(values, gain, bias):
    average = jnp.mean(values, axis=-1, keepdims=True)
    centred = values - average
    inverse = lax.rsqrt(jnp.mean(centred * centred, axis=-1, keepdims=True) + EPS)
    unit_rows = centred * inverse
    return (unit_rows * gain + bias, unit_rows, inverse)


def normalize_back(gradient, unit_rows, inverse, gain):
    scaled = gradient * gain
    inner_sum = (
        scaled
        - jnp.mean(scaled, axis=-1, keepdims=True)
        - unit_rows * jnp.mean(scaled * unit_rows, axis=-1, keepdims=True)
    )
    return (inner_sum * inverse, jnp.sum(gradient * unit_rows, axis=0), jnp.sum(gradient, axis=0))


def rows_in(values):
    return lax.all_gather(values, "head", axis=0, tiled=True)


def grads_in(values):
    return lax.all_gather(values, "head", axis=0, tiled=True)


def branch_sum(left_op, right_op):
    return lax.psum_scatter(
        jnp.dot(left_op, right_op, preferred_element_type=jnp.float32),
        "head",
        scatter_dimension=0,
        tiled=True,
    )


def input_sum(operand_pairs):
    summed = None
    for left_op, right_op in operand_pairs:
        partial_value = lax.dot_general(
            left_op, right_op, (((1,), (1,)), ((), ())), preferred_element_type=jnp.float32
        )
        summed = partial_value if summed is None else summed + partial_value
    return lax.psum_scatter(summed, "head", scatter_dimension=0, tiled=True)


def masked_scores(rows_q, key_heads, first_row, score_scale):
    scores = (
        jnp.einsum("qgd,kgd->gqk", rows_q, key_heads, preferred_element_type=jnp.float32)
        * score_scale
    )
    place_q = first_row + jnp.arange(rows_q.shape[0], dtype=jnp.int32)
    place_k = jnp.arange(key_heads.shape[0], dtype=jnp.int32)
    allowed = place_k[None, :] <= place_q[:, None]
    return jnp.where(allowed[None], scores, -1e30)


def attend(queries, key_rows, value_rows, block_rows):
    length, width = queries.shape
    groups = width // HD
    score_scale = 1.0 / math.sqrt(HD)
    query_heads = queries.reshape(length, groups, HD)
    key_heads = key_rows.reshape(length, groups, HD)
    value_heads = value_rows.reshape(length, groups, HD)
    out_blocks = []
    totals = []
    for position in range(length // block_rows):
        first_row = position * block_rows
        last_row = first_row + block_rows
        scores = masked_scores(
            query_heads[first_row:last_row], key_heads[:last_row], first_row, score_scale
        )
        row_max = jnp.max(scores, axis=-1, keepdims=True)
        exp_scores = jnp.exp(scores - row_max)
        row_total = jnp.sum(exp_scores, axis=-1, keepdims=True)
        weights = (exp_scores / row_total).astype(jnp.bfloat16)
        out_blocks.append(
            jnp.einsum(
                "gqk,kgd->qgd", weights, value_heads[:last_row], preferred_element_type=jnp.float32
            )
        )
        totals.append(row_max + jnp.log(row_total))
    return (jnp.concatenate(out_blocks, axis=0).reshape(length, width), totals)


def attend_back(queries, key_rows, value_rows, grad_rows, totals, block_rows):
    length, width = queries.shape
    groups = width // HD
    score_scale = 1.0 / math.sqrt(HD)
    query_heads = queries.reshape(length, groups, HD)
    key_heads = key_rows.reshape(length, groups, HD)
    value_heads = value_rows.reshape(length, groups, HD)
    grad_heads = grad_rows.reshape(length, groups, HD)
    grad_keys = jnp.zeros((length, groups, HD), jnp.float32)
    grad_values = jnp.zeros((length, groups, HD), jnp.float32)
    query_parts = []
    for position in range(length // block_rows):
        first_row = position * block_rows
        last_row = first_row + block_rows
        rows_q = query_heads[first_row:last_row]
        scores = masked_scores(rows_q, key_heads[:last_row], first_row, score_scale)
        weights = jnp.exp(scores - totals[position])
        rounded = weights.astype(jnp.bfloat16)
        grad_block = grad_heads[first_row:last_row]
        grad_values = grad_values.at[:last_row].add(
            jnp.einsum("gqk,qgd->kgd", rounded, grad_block, preferred_element_type=jnp.float32)
        )
        grad_weights = jnp.einsum(
            "qgd,kgd->gqk", grad_block, value_heads[:last_row], preferred_element_type=jnp.float32
        )
        inner_sum = jnp.sum(weights * grad_weights, axis=-1, keepdims=True)
        grad_scores = (weights * (grad_weights - inner_sum)).astype(jnp.bfloat16)
        query_parts.append(
            jnp.einsum(
                "gqk,kgd->qgd",
                grad_scores,
                key_heads[:last_row],
                preferred_element_type=jnp.float32,
            )
            * score_scale
        )
        grad_keys = grad_keys.at[:last_row].add(
            jnp.einsum("gqk,qgd->kgd", grad_scores, rows_q, preferred_element_type=jnp.float32)
            * score_scale
        )
    grad_queries = jnp.concatenate(query_parts, axis=0).reshape(length, width).astype(jnp.bfloat16)
    return (
        grad_queries,
        grad_keys.reshape(length, width).astype(jnp.bfloat16),
        grad_values.reshape(length, width).astype(jnp.bfloat16),
    )


def contract_rows(left_op, right_op):
    return lax.dot_general(
        left_op, right_op, (((0,), (0,)), ((), ())), preferred_element_type=jnp.float32
    )


def contract_cols(left_op, right_op):
    return lax.dot_general(
        left_op, right_op, (((1,), (1,)), ((), ())), preferred_element_type=jnp.float32
    )


def on_device(
    tokens, cotangent, w_query, w_key, w_value, w_out, w_up, w_down, norm_gain, norm_bias
):
    full_q, full_k, full_v, full_o, full_up, full_down = (
        lax.all_gather(w_query, "wide", axis=0, tiled=True),
        lax.all_gather(w_key, "wide", axis=0, tiled=True),
        lax.all_gather(w_value, "wide", axis=0, tiled=True),
        lax.all_gather(w_out, "wide", axis=1, tiled=True),
        lax.all_gather(w_up, "wide", axis=0, tiled=True),
        lax.all_gather(w_down, "wide", axis=1, tiled=True),
    )
    residual = tokens.astype(jnp.float32)
    norm_a, unit_a, inv_a = normalize(residual, norm_gain[0], norm_bias[0])
    seq_a = rows_in(norm_a.astype(jnp.bfloat16))
    block_rows = min(512, seq_a.shape[0])
    queries = jnp.dot(seq_a, full_q, preferred_element_type=jnp.float32).astype(jnp.bfloat16)
    key_rows = jnp.dot(seq_a, full_k, preferred_element_type=jnp.float32).astype(jnp.bfloat16)
    value_rows = jnp.dot(seq_a, full_v, preferred_element_type=jnp.float32).astype(jnp.bfloat16)
    attended, totals = attend(queries, key_rows, value_rows, block_rows)
    attended = attended.astype(jnp.bfloat16)
    mixed = branch_sum(attended, full_o)
    norm_z, unit_z, inv_z = normalize(mixed, norm_gain[1], norm_bias[1])
    hidden = residual + norm_z
    norm_c, unit_c, inv_c = normalize(hidden, norm_gain[2], norm_bias[2])
    seq_c = rows_in(norm_c.astype(jnp.bfloat16))
    pre_act = jnp.dot(seq_c, full_up, preferred_element_type=jnp.float32)
    active, gelu_back = jax.vjp(jax.nn.gelu, pre_act)
    active = active.astype(jnp.bfloat16)
    output = branch_sum(active, full_down)
    norm_m, unit_m, inv_m = normalize(output, norm_gain[3], norm_bias[3])
    block_out = (hidden + norm_m).astype(jnp.bfloat16)
    full_q, full_k, full_v, full_o, full_up, full_down = (
        lax.all_gather(w_query, "wide", axis=0, tiled=True),
        lax.all_gather(w_key, "wide", axis=0, tiled=True),
        lax.all_gather(w_value, "wide", axis=0, tiled=True),
        lax.all_gather(w_out, "wide", axis=1, tiled=True),
        lax.all_gather(w_up, "wide", axis=0, tiled=True),
        lax.all_gather(w_down, "wide", axis=1, tiled=True),
    )
    grad_y = cotangent.astype(jnp.float32)
    grad_m, gain_m, bias_m = normalize_back(grad_y, unit_m, inv_m, norm_gain[3])
    seq_gm = grads_in(grad_m.astype(jnp.bfloat16))
    grad_act = contract_cols(seq_gm, full_down)
    grad_pre = gelu_back(grad_act)[0].astype(jnp.bfloat16)
    grad_down = contract_rows(active, seq_gm)
    grad_up = contract_rows(seq_c, grad_pre)
    grad_c = input_sum(((grad_pre, full_up),))
    grad_more, gain_c, bias_c = normalize_back(grad_c, unit_c, inv_c, norm_gain[2])
    grad_h = grad_y + grad_more
    grad_z, gain_z, bias_z = normalize_back(grad_h, unit_z, inv_z, norm_gain[1])
    seq_gz = grads_in(grad_z.astype(jnp.bfloat16))
    grad_att = contract_cols(seq_gz, full_o).astype(jnp.bfloat16)
    grad_o = contract_rows(attended, seq_gz)
    grad_queries, grad_keys, grad_values = attend_back(
        queries, key_rows, value_rows, grad_att, totals, block_rows
    )
    grad_q = contract_rows(seq_a, grad_queries)
    grad_k = contract_rows(seq_a, grad_keys)
    grad_v = contract_rows(seq_a, grad_values)
    grad_a = input_sum(((grad_queries, full_q), (grad_keys, full_k), (grad_values, full_v)))
    grad_first, gain_a, bias_a = normalize_back(grad_a, unit_a, inv_a, norm_gain[0])
    input_grad = grad_h + grad_first
    grad_q, grad_k, grad_v, grad_o, grad_up, grad_down = (
        lax.psum_scatter(grad_q, "wide", scatter_dimension=0, tiled=True),
        lax.psum_scatter(grad_k, "wide", scatter_dimension=0, tiled=True),
        lax.psum_scatter(grad_v, "wide", scatter_dimension=0, tiled=True),
        lax.psum_scatter(grad_o, "wide", scatter_dimension=1, tiled=True),
        lax.psum_scatter(grad_up, "wide", scatter_dimension=0, tiled=True),
        lax.psum_scatter(grad_down, "wide", scatter_dimension=1, tiled=True),
    )
    gain_grad, bias_grad = lax.psum(
        (jnp.stack([gain_a, gain_z, gain_c, gain_m]), jnp.stack([bias_a, bias_z, bias_c, bias_m])),
        ("wide", "head"),
    )
    return (
        block_out,
        input_grad,
        grad_q,
        grad_k,
        grad_v,
        grad_o,
        grad_up,
        grad_down,
        gain_grad,
        bias_grad,
    )


def solution(mesh):
    in_specs = (
        P(("wide", "head"), None),
        P(("wide", "head"), None),
        P("wide", "head"),
        P("wide", "head"),
        P("wide", "head"),
        P("head", "wide"),
        P("wide", "head"),
        P("head", "wide"),
        P(),
        P(),
    )
    out_specs = (
        P(("wide", "head"), None),
        P(("wide", "head"), None),
        P("wide", "head"),
        P("wide", "head"),
        P("wide", "head"),
        P("head", "wide"),
        P("wide", "head"),
        P("head", "wide"),
        P(),
        P(),
    )
    return jax.shard_map(
        on_device, mesh=mesh, in_specs=in_specs, out_specs=out_specs, check_vma=False
    )
```

profile of v0, /device:TPU:0, one launch (start us, length us, event | category | flops | bytes accessed | tf_op | source)
XLA Modules:
  0.0 1443.2 jit_solution(8579794204711242059)
XLA Ops:
  15.8 12.4 all_gather.38
  47.9 11.1 all_gather.40
  63.0 36.4 %all-gather.7.cloned.1.call-done = bf16[2048,1024]{1,0:T(8,128)(2,1)} async-done(((bf16[512,1024]{1,0:T(8,128)(2,1)}), bf16[2048,1024]{1,0:T(8,128)(2,1)}) %all-gather.7.cloned.1.call-update) | async-done | bytes 4194320 | tf_op jit(solution)/shard_map/all_gather | solution.py:33
  159.6 142.6 %reduce-scatter.11.cloned.1.call-done = f32[512,1024]{1,0:T(8,128)} async-done(((f32[2048,1024]{1,0:T(8,128)}), f32[512,1024]{1,0:T(8,128)}) %reduce-scatter.11.cloned.1.call-update) | async-done | bytes 2097168 | tf_op jit(solution)/shard_map/reduce_scatter | solution.py:41
  310.9 80.5 %all-gather.9.cloned.1.call-done = bf16[2048,1024]{1,0:T(8,128)(2,1)} async-done(((bf16[512,1024]{1,0:T(8,128)(2,1)}), bf16[2048,1024]{1,0:T(8,128)(2,1)}) %all-gather.9.cloned.1.call-update) | async-done | bytes 4194320 | tf_op jit(solution)/shard_map/all_gather | solution.py:33
  391.4 10.6 fusion.121
  402.0 17.6 %all-gather.13.cloned.1.call-done = bf16[1024,1024]{1,0:T(8,128)(2,1)} async-done(((bf16[1024,128]{1,0:T(8,128)(2,1)}), bf16[1024,1024]{1,0:T(8,128)(2,1)}) %all-gather.13.cloned.1.call-update) | async-done | bytes 2097168 | tf_op jit(solution)/shard_map/all_gather | solution.py:167
  419.6 12.7 fusion.110
  432.4 144.6 %reduce-scatter.13.cloned.1.call-done = f32[512,1024]{1,0:T(8,128)} async-done(((f32[2048,1024]{1,0:T(8,128)}), f32[512,1024]{1,0:T(8,128)}) %reduce-scatter.13.cloned.1.call-update) | async-done | bytes 2097168 | tf_op jit(solution)/shard_map/reduce_scatter | solution.py:41
  586.8 81.0 %all-gather.15.cloned.1.call-done = bf16[2048,1024]{1,0:T(8,128)(2,1)} async-done(((bf16[512,1024]{1,0:T(8,128)(2,1)}), bf16[2048,1024]{1,0:T(8,128)(2,1)}) %all-gather.15.cloned.1.call-update) | async-done | bytes 4194320 | tf_op jit(solution)/shard_map/all_gather | solution.py:37
  667.8 12.6 fusion.10
  689.4 143.1 %reduce-scatter.15.cloned.1.call-done = f32[512,1024]{1,0:T(8,128)} async-done(((f32[2048,1024]{1,0:T(8,128)}), f32[512,1024]{1,0:T(8,128)}) %reduce-scatter.15.cloned.1.call-update) | async-done | bytes 2097168 | tf_op jit(solution)/shard_map/reduce_scatter | solution.py:56
  841.6 81.2 %all-gather.17.cloned.1.call-done = bf16[2048,1024]{1,0:T(8,128)(2,1)} async-done(((bf16[512,1024]{1,0:T(8,128)(2,1)}), bf16[2048,1024]{1,0:T(8,128)(2,1)}) %all-gather.17.cloned.1.call-update) | async-done | bytes 4194320 | tf_op jit(solution)/shard_map/all_gather | solution.py:37
  938.6 11.1 multiply_reduce_fusion.1
  998.0 10.4 multiply_convert_fusion
  1024.3 10.1 fusion.129
  1034.5 12.1 fusion.109
  1066.9 100.1 %reduce-scatter.17.cloned.1.call-done = f32[512,1024]{1,0:T(8,128)} async-done(((f32[2048,1024]{1,0:T(8,128)}), f32[512,1024]{1,0:T(8,128)}) %reduce-scatter.17.cloned.1.call-update) | async-done | bytes 2097168 | tf_op jit(solution)/shard_map/reduce_scatter | solution.py:56
  1169.7 41.8 %all-reduce.2 = (f32[4,1024]{1,0:T(4,128)}, f32[4,1024]{1,0:T(4,128)}) all-reduce(f32[4,1024]{1,0:T(4,128)S(1)} %pad_maximum_fusion.2, f32[4,1024]{1,0:T(4,128)S(1)} %pad_maximum_fusion.3), channel_id=1, replica_groups=mesh['wide'=8,'head'=4] {'wide','head'}, use_global_device_ids=true, to_apply=%region_42.43 | all-reduce | flops 8192 | bytes 65536 | tf_op jit(solution)/shard_map/psum | solution.py:228
  1222.7 54.7 %reduce-scatter.29.cloned.1.call-done = f32[1024,128]{1,0:T(8,128)} async-done(((f32[1024,1024]{1,0:T(8,128)}), f32[1024,128]{1,0:T(8,128)}) %reduce-scatter.29.cloned.1.call-update) | async-done | bytes 524304 | tf_op jit(solution)/shard_map/reduce_scatter | solution.py:226
  1277.5 39.5 %reduce-scatter.25.cloned.1.call-done = f32[256,128]{1,0:T(8,128)} async-done(((f32[256,1024]{1,0:T(8,128)}), f32[256,128]{1,0:T(8,128)}) %reduce-scatter.25.cloned.1.call-update) | async-done | bytes 131088 | tf_op jit(solution)/shard_map/reduce_scatter | solution.py:224
  1317.0 39.7 %reduce-scatter.23.cloned.1.call-done = f32[128,256]{1,0:T(8,128)} async-done(((f32[1024,256]{1,0:T(8,128)}), f32[128,256]{1,0:T(8,128)}) %reduce-scatter.23.cloned.1.call-update) | async-done | bytes 131088 | tf_op jit(solution)/shard_map/reduce_scatter | solution.py:223
  1356.7 39.5 %reduce-scatter.21.cloned.1.call-done = f32[128,256]{1,0:T(8,128)} async-done(((f32[1024,256]{1,0:T(8,128)}), f32[128,256]{1,0:T(8,128)}) %reduce-scatter.21.cloned.1.call-update) | async-done | bytes 131088 | tf_op jit(solution)/shard_map/reduce_scatter | solution.py:222
  1396.2 39.7 %reduce-scatter.19.cloned.1.call-done = f32[128,256]{1,0:T(8,128)} async-done(((f32[1024,256]{1,0:T(8,128)}), f32[128,256]{1,0:T(8,128)}) %reduce-scatter.19.cloned.1.call-update) | async-done | bytes 131088 | tf_op jit(solution)/shard_map/reduce_scatter | solution.py:221
  (315 shorter events, 241.2 us)
Async XLA Ops:
  8.0 91.3 %all-gather.7.cloned.1.call-start = ((), (), s32[]{:S(2)}) async-start(), calls=%async_computation.10 | async-start | bytes 5242880 | tf_op jit(solution)/shard_map/all_gather | solution.py:33
  15.7 286.6 %reduce-scatter.11.cloned.1.call-start = ((), (), s32[]{:S(2)}) async-start(), calls=%async_computation.11 | async-start | bytes 10485760 | tf_op jit(solution)/shard_map/reduce_scatter | solution.py:41
  159.0 147.0 %copy-start.7 = (bf16[512,1024]{1,0:T(8,128)(2,1)S(1)}, bf16[512,1024]{1,0:T(8,128)(2,1)}, u32[]{:S(2)}) copy-start(bf16[512,1024]{1,0:T(8,128)(2,1)} %param.30) | copy-start | bytes 3145732
  159.0 151.9 %all-gather.11.cloned.1.call-start = ((), (), s32[]{:S(2)}) async-start(), calls=%async_computation.13 | async-start | bytes 2359296 | tf_op jit(solution)/shard_map/all_gather | solution.py:166
  159.6 231.8 %all-gather.9.cloned.1.call-start = ((), (), s32[]{:S(2)}) async-start(), calls=%async_computation.12 | async-start | bytes 5242880 | tf_op jit(solution)/shard_map/all_gather | solution.py:33
  310.1 109.6 %all-gather.13.cloned.1.call-start = ((), (), s32[]{:S(2)}) async-start(), calls=%async_computation.14 | async-start | bytes 2359296 | tf_op jit(solution)/shard_map/all_gather | solution.py:167
  310.7 266.4 %reduce-scatter.13.cloned.1.call-start = ((), (), s32[]{:S(2)}) async-start(), calls=%async_computation.15 | async-start | bytes 10485760 | tf_op jit(solution)/shard_map/reduce_scatter | solution.py:41
  432.3 148.6 %copy-start.17 = (bf16[512,1024]{1,0:T(8,128)(2,1)S(1)}, bf16[512,1024]{1,0:T(8,128)(2,1)}, u32[]{:S(2)}) copy-start(bf16[512,1024]{1,0:T(8,128)(2,1)} %param.31) | copy-start | bytes 3145732
  432.4 235.4 %all-gather.15.cloned.1.call-start = ((), (), s32[]{:S(2)}) async-start(), calls=%async_computation.16 | async-start | bytes 5242880 | tf_op jit(solution)/shard_map/all_gather | solution.py:37
  586.3 246.2 %reduce-scatter.15.cloned.1.call-start = ((), (), s32[]{:S(2)}) async-start(), calls=%async_computation.17 | async-start | bytes 10485760 | tf_op jit(solution)/shard_map/reduce_scatter | solution.py:56
  689.4 233.5 %all-gather.17.cloned.1.call-start = ((), (), s32[]{:S(2)}) async-start(), calls=%async_computation.18 | async-start | bytes 5242880 | tf_op jit(solution)/shard_map/all_gather | solution.py:37
  841.5 325.5 %reduce-scatter.17.cloned.1.call-start = ((), (), s32[]{:S(2)}) async-start(), calls=%async_computation.19 | async-start | bytes 10485760 | tf_op jit(solution)/shard_map/reduce_scatter | solution.py:56
  1023.8 198.9 %reduce-scatter.27.cloned.1.call-start = ((), (), s32[]{:S(2)}) async-start(), calls=%async_computation.24 | async-start | bytes 4718592 | tf_op jit(solution)/shard_map/reduce_scatter | solution.py:225
  1034.4 243.1 %reduce-scatter.29.cloned.1.call-start = ((), (), s32[]{:S(2)}) async-start(), calls=%async_computation.25 | async-start | bytes 4718592 | tf_op jit(solution)/shard_map/reduce_scatter | solution.py:226
  1046.6 270.4 %reduce-scatter.25.cloned.1.call-start = ((), (), s32[]{:S(2)}) async-start(), calls=%async_computation.23 | async-start | bytes 1179648 | tf_op jit(solution)/shard_map/reduce_scatter | solution.py:224
  1052.3 304.4 %reduce-scatter.23.cloned.1.call-start = ((), (), s32[]{:S(2)}) async-start(), calls=%async_computation.22 | async-start | bytes 1179648 | tf_op jit(solution)/shard_map/reduce_scatter | solution.py:223
  1057.2 339.1 %reduce-scatter.21.cloned.1.call-start = ((), (), s32[]{:S(2)}) async-start(), calls=%async_computation.21 | async-start | bytes 1179648 | tf_op jit(solution)/shard_map/reduce_scatter | solution.py:222
  1062.0 105.0 %copy-start.8 = (bf16[512,1024]{1,0:T(8,128)(2,1)S(1)}, bf16[512,1024]{1,0:T(8,128)(2,1)}, u32[]{:S(2)}) copy-start(bf16[512,1024]{1,0:T(8,128)(2,1)} %param.30) | copy-start | bytes 3145732
  1062.0 105.0 %copy-start.59 = (f32[1,1024]{1,0:T(1,128)S(1)}, f32[1,1024]{1,0:T(1,128)}, u32[]{:S(2)}) copy-start(f32[1,1024]{1,0:T(1,128)} %copy-done.58) | copy-start | bytes 12292
  1062.1 105.0 %copy-start.65 = (f32[512]{0:T(512)S(1)}, f32[512]{0:T(512)}, u32[]{:S(2)}) copy-start(f32[512]{0:T(512)} %copy-done.64) | copy-start | bytes 6148
  1062.1 105.0 %copy-start.68 = (f32[512]{0:T(512)S(1)}, f32[512]{0:T(512)}, u32[]{:S(2)}) copy-start(f32[512]{0:T(512)} %copy-done.67) | copy-start | bytes 6148
  1062.1 373.9 %reduce-scatter.19.cloned.1.call-start = ((), (), s32[]{:S(2)}) async-start(), calls=%async_computation.20 | async-start | bytes 1179648 | tf_op jit(solution)/shard_map/reduce_scatter | solution.py:221
  1066.8 102.8 %copy-start.71 = (f32[1024]{0:T(1024)S(1)}, f32[1024]{0:T(1024)}, u32[]{:S(2)}) copy-start(f32[1024]{0:T(1024)} %get-tuple-element.135) | copy-start | bytes 12292
  1066.8 144.7 %copy-start.12 = (f32[512,1024]{1,0:T(8,128)S(1)}, f32[512,1024]{1,0:T(8,128)}, u32[]{:S(2)}) copy-start(f32[512,1024]{1,0:T(8,128)} %copy-done.11) | copy-start | bytes 6291460
  (79 other events, 1299.1 us)
Sparse Core Ops, SparseCore 0:
  15.8 83.4 all-gather.6
  159.1 143.0 reduce-scatter.10
  586.4 81.2 all-gather.14
  689.5 143.0 reduce-scatter.14
Sparse Core Ops, SparseCore 1:
  161.4 26.1 all-gather.10
  310.2 81.2 all-gather.8
  393.2 26.4 all-gather.12
  432.4 144.6 reduce-scatter.12
  841.6 81.2 all-gather.16
  1023.9 143.1 reduce-scatter.16
  1170.8 51.9 reduce-scatter.26
  1226.5 50.9 reduce-scatter.28
  1281.1 35.9 reduce-scatter.24
  1320.8 35.9 reduce-scatter.22
  1360.3 35.9 reduce-scatter.20
  1400.0 35.9 reduce-scatter.18
where the time goes:
time: 1450 us; the launch traced here: 1440 us
  waiting for transfers between devices  1050 us (72%)
  matrix products  193 us (13%)
  blocking collectives  85 us (6%)
  other arithmetic  81.8 us (6%)
  between operations  16.8 us (1%)
  local copies, waits for them, and re-layouts  15.2 us (1%)
    reduce_scatter x2, waiting for transfers between devices, branch_sum(): lax.psum_scatter(jnp.dot(left_op, right_op, preferred_element_type=jnp.fl...  287 us
    reduce_scatter x2, waiting for transfers between devices, input_sum(): return lax.psum_scatter(summed, 'head', scatter_dimension=0, tiled=True)  243 us
    all_gather x2, waiting for transfers between devices, grads_in(): return lax.all_gather(values, 'head', axis=0, tiled=True)  162 us
    all_gather x2, waiting for transfers between devices, rows_in(): return lax.all_gather(values, 'head', axis=0, tiled=True)  117 us
    reduce_scatter x1, waiting for transfers between devices, on_device(): lax.psum_scatter(grad_down, 'wide', scatter_dimension=1, tiled=True)  54.7 us
    psum x1, blocking collectives, on_device(): lax.psum((jnp.stack([gain_a, gain_z, gain_c, gain_m]), jnp.stack([bias_a,...  41.8 us
    dot_general x6, matrix products, contract_rows(): lax.dot_general(left_op, right_op, (((0,), (0,)), ((), ())), preferred_el...  40.8 us
    reduce_scatter x1, waiting for transfers between devices, on_device(): lax.psum_scatter(grad_v, 'wide', scatter_dimension=0, tiled=True)  39.7 us
  transfers between devices with their start and end apart: 16, of which 15 were waited for; matrix products, arithmetic and copies ran while one was open for 5% of the time, Pallas kernels for 0%

commit v1 on v0

v1 whole, which is shorter than its diff:
```python
import math

import jax
import jax.numpy as jnp
from jax import lax
from jax.sharding import Mesh, PartitionSpec as P

HD = 64


EPS = 1e-05


def normalize(values, gain, bias):
    average = jnp.mean(values, axis=-1, keepdims=True)
    centred = values - average
    inverse = lax.rsqrt(jnp.mean(centred * centred, axis=-1, keepdims=True) + EPS)
    unit_rows = centred * inverse
    return (unit_rows * gain + bias, unit_rows, inverse)


def normalize_back(gradient, unit_rows, inverse, gain):
    scaled = gradient * gain
    inner_sum = (
        scaled
        - jnp.mean(scaled, axis=-1, keepdims=True)
        - unit_rows * jnp.mean(scaled * unit_rows, axis=-1, keepdims=True)
    )
    return (inner_sum * inverse, jnp.sum(gradient * unit_rows, axis=0), jnp.sum(gradient, axis=0))


def masked_scores(rows_q, key_heads, first_row, score_scale):
    scores = (
        jnp.einsum("qgd,kgd->gqk", rows_q, key_heads, preferred_element_type=jnp.float32)
        * score_scale
    )
    place_q = first_row + jnp.arange(rows_q.shape[0], dtype=jnp.int32)
    place_k = jnp.arange(key_heads.shape[0], dtype=jnp.int32)
    allowed = place_k[None, :] <= place_q[:, None]
    return jnp.where(allowed[None], scores, -1e30)


def attend(queries, key_rows, value_rows, block_rows):
    length, width = queries.shape
    groups = width // HD
    score_scale = 1.0 / math.sqrt(HD)
    query_heads = queries.reshape(length, groups, HD)
    key_heads = key_rows.reshape(length, groups, HD)
    value_heads = value_rows.reshape(length, groups, HD)
    out_blocks = []
    totals = []
    for position in range(length // block_rows):
        first_row = position * block_rows
        last_row = first_row + block_rows
        scores = masked_scores(
            query_heads[first_row:last_row], key_heads[:last_row], first_row, score_scale
        )
        row_max = jnp.max(scores, axis=-1, keepdims=True)
        exp_scores = jnp.exp(scores - row_max)
        row_total = jnp.sum(exp_scores, axis=-1, keepdims=True)
        weights = (exp_scores / row_total).astype(jnp.bfloat16)
        out_blocks.append(
            jnp.einsum(
                "gqk,kgd->qgd", weights, value_heads[:last_row], preferred_element_type=jnp.float32
            )
        )
        totals.append(row_max + jnp.log(row_total))
    return (jnp.concatenate(out_blocks, axis=0).reshape(length, width), totals)


def attend_back(queries, key_rows, value_rows, grad_rows, totals, block_rows):
    length, width = queries.shape
    groups = width // HD
    score_scale = 1.0 / math.sqrt(HD)
    query_heads = queries.reshape(length, groups, HD)
    key_heads = key_rows.reshape(length, groups, HD)
    value_heads = value_rows.reshape(length, groups, HD)
    grad_heads = grad_rows.reshape(length, groups, HD)
    grad_keys = jnp.zeros((length, groups, HD), jnp.float32)
    grad_values = jnp.zeros((length, groups, HD), jnp.float32)
    query_parts = []
    for position in range(length // block_rows):
        first_row = position * block_rows
        last_row = first_row + block_rows
        rows_q = query_heads[first_row:last_row]
        scores = masked_scores(rows_q, key_heads[:last_row], first_row, score_scale)
        weights = jnp.exp(scores - totals[position])
        rounded = weights.astype(jnp.bfloat16)
        grad_block = grad_heads[first_row:last_row]
        grad_values = grad_values.at[:last_row].add(
            jnp.einsum("gqk,qgd->kgd", rounded, grad_block, preferred_element_type=jnp.float32)
        )
        grad_weights = jnp.einsum(
            "qgd,kgd->gqk", grad_block, value_heads[:last_row], preferred_element_type=jnp.float32
        )
        inner_sum = jnp.sum(weights * grad_weights, axis=-1, keepdims=True)
        grad_scores = (weights * (grad_weights - inner_sum)).astype(jnp.bfloat16)
        query_parts.append(
            jnp.einsum(
                "gqk,kgd->qgd",
                grad_scores,
                key_heads[:last_row],
                preferred_element_type=jnp.float32,
            )
            * score_scale
        )
        grad_keys = grad_keys.at[:last_row].add(
            jnp.einsum("gqk,qgd->kgd", grad_scores, rows_q, preferred_element_type=jnp.float32)
            * score_scale
        )
    grad_queries = jnp.concatenate(query_parts, axis=0).reshape(length, width).astype(jnp.bfloat16)
    return (
        grad_queries,
        grad_keys.reshape(length, width).astype(jnp.bfloat16),
        grad_values.reshape(length, width).astype(jnp.bfloat16),
    )


def contract_rows(left_op, right_op):
    return lax.dot_general(
        left_op, right_op, (((0,), (0,)), ((), ())), preferred_element_type=jnp.float32
    )


def contract_cols(left_op, right_op):
    return lax.dot_general(
        left_op, right_op, (((1,), (1,)), ((), ())), preferred_element_type=jnp.float32
    )

WIDE = ("outer", "pair")
ALL = ("outer", "pair", "head")


def swap(values):
    return lax.ppermute(values, "pair", [(0, 1), (1, 0)])


def halves(block, axis):
    size = block.shape[axis] // 2
    place = lax.axis_index("pair")
    own = lax.dynamic_slice_in_dim(block, place * size, size, axis)
    other = lax.dynamic_slice_in_dim(block, (1 - place) * size, size, axis)
    return own, other


def in_order(own, other, axis):
    place = lax.axis_index("pair")
    return jnp.where(
        place == 0,
        jnp.concatenate([own, other], axis=axis),
        jnp.concatenate([other, own], axis=axis),
    )


def gather_half(block):
    own, other = halves(block, 1)
    pair_rows = in_order(own, swap(other), 0)
    columns = lax.all_gather(pair_rows, "head", axis=0, tiled=False)
    columns = columns.transpose(1, 0, 2).reshape(pair_rows.shape[0], -1)
    return lax.all_gather(columns, "outer", axis=0, tiled=True)


def scatter_half(grad, groups):
    rows = lax.psum_scatter(grad, "outer", scatter_dimension=0, tiled=True)
    blocks = rows.reshape(rows.shape[0], groups, -1).transpose(1, 0, 2)
    block = lax.psum_scatter(blocks, "head", scatter_dimension=0, tiled=False)
    own, other = halves(block, 0)
    return in_order(own, swap(other), 1)


def on_device(
    tokens, cotangent, w_query, w_key, w_value, w_out, w_up, w_down, norm_gain, norm_bias
):
    groups = lax.axis_size("head")
    rows = tokens.shape[0]
    width = w_query.shape[1]
    bf16 = jnp.bfloat16
    w_attn = lax.all_gather(
        jnp.concatenate([w_query, w_key, w_value], axis=1), WIDE, axis=0, tiled=True
    )
    residual = tokens.astype(jnp.float32)
    norm_a, unit_a, inv_a = normalize(residual, norm_gain[0], norm_bias[0])
    seq_a = lax.all_gather(norm_a.astype(bf16), "head", axis=0, tiled=True)
    full_o = lax.all_gather(
        lax.all_gather(w_out, "head", axis=0, tiled=True).T, WIDE, axis=0, tiled=True
    )
    full_up = gather_half(w_up)
    full_down = gather_half(w_down.T)
    block_rows = min(512, seq_a.shape[0])
    qkv = jnp.dot(seq_a, w_attn, preferred_element_type=jnp.float32).astype(bf16)
    queries, key_rows, value_rows = (qkv[:, i * width : (i + 1) * width] for i in range(3))
    attended, totals = attend(queries, key_rows, value_rows, block_rows)
    attended = lax.all_to_all(
        attended.astype(bf16).reshape(groups, rows, width), "head", 0, 0, tiled=False
    )
    attended = attended.transpose(1, 0, 2).reshape(rows, groups * width)
    mixed = contract_cols(attended, full_o)
    norm_z, unit_z, inv_z = normalize(mixed, norm_gain[1], norm_bias[1])
    hidden = residual + norm_z
    norm_c, unit_c, inv_c = normalize(hidden, norm_gain[2], norm_bias[2])
    rows_c = norm_c.astype(bf16)
    pair_c = jnp.concatenate([rows_c, swap(rows_c)], axis=0)
    pre_act = jnp.dot(pair_c, full_up, preferred_element_type=jnp.float32)
    active, gelu_back = jax.vjp(jax.nn.gelu, pre_act)
    active = active.astype(bf16)
    both = contract_cols(active, full_down)
    output = both[:rows] + swap(both[rows:].astype(bf16)).astype(jnp.float32)
    norm_m, unit_m, inv_m = normalize(output, norm_gain[3], norm_bias[3])
    block_out = (hidden + norm_m).astype(bf16)
    grad_y = cotangent.astype(jnp.float32)
    grad_m, gain_m, bias_m = normalize_back(grad_y, unit_m, inv_m, norm_gain[3])
    rows_gm = grad_m.astype(bf16)
    pair_gm = jnp.concatenate([rows_gm, swap(rows_gm)], axis=0)
    grad_act = jnp.dot(pair_gm, full_down, preferred_element_type=jnp.float32)
    grad_pre = gelu_back(grad_act)[0].astype(bf16)
    both_c = contract_cols(grad_pre, full_up)
    grad_c = both_c[:rows] + swap(both_c[rows:].astype(bf16)).astype(jnp.float32)
    grad_down = scatter_half(contract_rows(pair_gm, active).astype(bf16), groups).T
    grad_up = scatter_half(contract_rows(pair_c, grad_pre).astype(bf16), groups)
    grad_more, gain_c, bias_c = normalize_back(grad_c, unit_c, inv_c, norm_gain[2])
    grad_h = grad_y + grad_more
    grad_z, gain_z, bias_z = normalize_back(grad_h, unit_z, inv_z, norm_gain[1])
    rows_gz = grad_z.astype(bf16)
    grad_att = jnp.dot(rows_gz, full_o, preferred_element_type=jnp.float32).astype(bf16)
    grad_att = grad_att.reshape(rows, groups, width).transpose(1, 0, 2)
    grad_att = lax.all_to_all(grad_att, "head", 0, 0, tiled=False)
    grad_att = grad_att.reshape(groups * rows, width)
    grad_o = contract_rows(rows_gz, attended).astype(bf16)
    grad_o = lax.psum_scatter(grad_o, WIDE, scatter_dimension=0, tiled=True)
    grad_o = grad_o.T.reshape(groups, width, -1)
    grad_o = lax.psum_scatter(grad_o, "head", scatter_dimension=0, tiled=False)
    grad_queries, grad_keys, grad_values = attend_back(
        queries, key_rows, value_rows, grad_att, totals, block_rows
    )
    grad_qkv = jnp.concatenate([grad_queries, grad_keys, grad_values], axis=1)
    grad_a = contract_cols(grad_qkv, w_attn).astype(bf16)
    grad_a = lax.psum_scatter(grad_a, "head", scatter_dimension=0, tiled=True).astype(jnp.float32)
    grad_w = contract_rows(seq_a, grad_qkv).astype(bf16)
    grad_w = lax.psum_scatter(grad_w, WIDE, scatter_dimension=0, tiled=True).astype(jnp.float32)
    grad_first, gain_a, bias_a = normalize_back(grad_a, unit_a, inv_a, norm_gain[0])
    input_grad = grad_h + grad_first
    gain_grad, bias_grad = lax.psum(
        (jnp.stack([gain_a, gain_z, gain_c, gain_m]), jnp.stack([bias_a, bias_z, bias_c, bias_m])),
        ALL,
    )
    return (
        block_out,
        input_grad,
        grad_w[:, :width],
        grad_w[:, width : 2 * width],
        grad_w[:, 2 * width :],
        grad_o.astype(jnp.float32),
        grad_up.astype(jnp.float32),
        grad_down.astype(jnp.float32),
        gain_grad,
        bias_grad,
    )


def solution(mesh):
    wide, head = mesh.shape["wide"], mesh.shape["head"]
    paired = Mesh(mesh.devices.reshape(wide // 2, 2, head), ALL)
    rows = P(ALL, None)
    by_rows = P(WIDE, "head")
    by_cols = P("head", WIDE)
    in_specs = (rows, rows, by_rows, by_rows, by_rows, by_cols, by_rows, by_cols, P(), P())
    out_specs = (rows, rows, by_rows, by_rows, by_rows, by_cols, by_rows, by_cols, P(), P())
    return jax.shard_map(
        on_device, mesh=paired, in_specs=in_specs, out_specs=out_specs, check_vma=False
    )
```

time: 1450 us -> 779 us (0.54)
  waiting for transfers between devices: 1050 us -> 378 us
  local copies, waits for them, and re-layouts: 15.2 us -> 48.2 us
  blocking collectives: 85 us -> 60.2 us
    reduce_scatter x10 -> x8, waiting for transfers between devices: 751 us -> 153 us  [the longest x1 71.6 us: on_device(): lax.psum_scatter(grad_a, 'head', scatter_dimension=0, tiled=True)]
    all_gather x6 -> x7, waiting for transfers between devices: 297 us -> 170 us  [the longest x1 82.8 us: on_device(): seq_a = lax.all_gather(norm_a.astype(bf16), 'head', axis=0, tiled=True)]
    all_to_all x0 -> x2, waiting for transfers between devices: none -> 42.1 us  [the longest x1 25.8 us: on_device(): lax.all_to_all(attended.astype(bf16).reshape(groups, rows, width), 'head'...]
    all_gather x4 -> x1, blocking collectives: 43.2 us -> 18.6 us  [on_device(): lax.all_gather(w_out, 'head', axis=0, tiled=True)]
    dot_general x10 -> x4, matrix products: 48.4 us -> 30.2 us  [the longest x1 11.2 us: on_device(): grad_act = jnp.dot(pair_gm, full_down, preferred_element_type=jnp.float32)]
    dot_general x6 -> x4, matrix products: 40.8 us -> 26.8 us  [contract_rows(): lax.dot_general(left_op, right_op, (((0,), (0,)), ((), ())), preferred_el...]
  transfers between devices with their start and end apart: 16 -> 25, of which waited for: 15 -> 17; matrix products, arithmetic and copies ran while one was open for 5% -> 32% of each run, Pallas kernels for 0% -> 0%
where the time goes in v1:
time: 779 us; the launch traced here: 776 us
  waiting for transfers between devices  378 us (49%)
  matrix products  190 us (24%)
  other arithmetic  73 us (9%)
  blocking collectives  60.2 us (8%)
  local copies, waits for them, and re-layouts  48.2 us (6%)
  between operations  15.3 us (2%)
  starting transfers between devices  11.2 us (1%)
    all_gather x1, waiting for transfers between devices, on_device(): seq_a = lax.all_gather(norm_a.astype(bf16), 'head', axis=0, tiled=True)  82.8 us
    reduce_scatter x1, waiting for transfers between devices, on_device(): lax.psum_scatter(grad_a, 'head', scatter_dimension=0, tiled=True)  71.6 us
    reduce_scatter x2, waiting for transfers between devices, scatter_half(): block = lax.psum_scatter(blocks, 'head', scatter_dimension=0, tiled=False)  42.9 us
    psum x1, blocking collectives, on_device(): lax.psum((jnp.stack([gain_a, gain_z, gain_c, gain_m]), jnp.stack([bias_a,...  41.5 us
    reduce_scatter x1, waiting for transfers between devices, on_device(): lax.psum_scatter(grad_w, WIDE, scatter_dimension=0, tiled=True)  38.3 us
    all_gather x2, waiting for transfers between devices, gather_half(): columns = lax.all_gather(pair_rows, 'head', axis=0, tiled=False)  31.8 us
    all_gather x2, waiting for transfers between devices, gather_half(): return lax.all_gather(columns, 'outer', axis=0, tiled=True)  31.1 us
    dot_general x4, matrix products, contract_rows(): lax.dot_general(left_op, right_op, (((0,), (0,)), ((), ())), preferred_el...  26.8 us
  transfers between devices with their start and end apart: 25, of which 17 were waited for; matrix products, arithmetic and copies ran while one was open for 32% of the time, Pallas kernels for 0%

profile of v1, /device:TPU:0, one launch (start us, length us, event | category | flops | bytes accessed | tf_op | source)
XLA Modules:
  0.0 775.5 jit_solution(3823945687830756972)
XLA Ops:
  18.0 18.6 %all_gather.28 = bf16[1024,128]{1,0:T(8,128)(2,1)} all-gather(bf16[256,128]{1,0:T(8,128)(2,1)S(1)} %copy-done.59), channel_id=1, replica_groups=mesh['outer'=4,'pair'=2,'head'=4] {'head'}, dimensions={0}, use_global_device_ids=true | all-gather | bytes 327680 | tf_op jit(solution)/shard_map/all_gather | solution.py:185
  36.7 9.3 %all-gather.14.cloned.1.call-done = bf16[4,256,512]{2,1,0:T(8,128)(2,1)} async-done(((bf16[1,256,512]{2,1,0:T(8,128)(2,1)}), bf16[4,256,512]{2,1,0:T(8,128)(2,1)}) %all-gather.14.cloned.1.call-update) | async-done | bytes 1048592 | tf_op jit(solution)/shard_map/all_gather | solution.py:158
  52.6 22.5 %all-gather.18.cloned.1.call-done = bf16[4,256,512]{2,1,0:T(8,128)(2,1)} async-done(((bf16[1,256,512]{2,1,0:T(8,128)(2,1)}), bf16[4,256,512]{2,1,0:T(8,128)(2,1)}) %all-gather.18.cloned.1.call-update) | async-done | bytes 1048592 | tf_op jit(solution)/shard_map/all_gather | solution.py:158
  77.4 24.6 %all-gather.10.cloned.1.call-done = bf16[1024,768]{1,0:T(8,128)(2,1)} async-done(((bf16[128,768]{1,0:T(8,128)(2,1)}), bf16[1024,768]{1,0:T(8,128)(2,1)}) %all-gather.10.cloned.1.call-update) | async-done | bytes 1572880 | tf_op jit(solution)/shard_map/all_gather | solution.py:178
  102.0 82.8 %all-gather.8.cloned.1.call-done = bf16[2048,1024]{1,0:T(8,128)(2,1)} async-done(((bf16[512,1024]{1,0:T(8,128)(2,1)}), bf16[2048,1024]{1,0:T(8,128)(2,1)}) %all-gather.8.cloned.1.call-update) | async-done | bytes 4194320 | tf_op jit(solution)/shard_map/all_gather | solution.py:183
  223.6 8.4 %fusion = f32[4,512]{1,0:T(4,128)S(1)} fusion(f32[4,512,2048]{2,1,0:T(8,128)} %get-tuple-element.223, f32[4,512]{1,0:T(4,128)S(1)} %get-tuple-element.222), kind=kLoop, calls=%fused_computation.6 | loop fusion | flops 8386560 | bytes 16793600 | tf_op jit(solution)/shard_map/reduce_sum | solution.py:60
  246.9 25.8 %all-to-all-done = bf16[4,512,256]{1,2,0:T(8,128)(2,1)S(1)} async-done(((bf16[4,512,256]{1,2,0:T(8,128)(2,1)}), bf16[4,512,256]{1,2,0:T(8,128)(2,1)S(1)}, u32[]{:S(2)}, u32[]{:S(2)}) %all-to-all-start) | async-done | bytes 1048608 | tf_op jit(solution)/shard_map/all_to_all | solution.py:193
  280.7 10.3 %fusion.85 = f32[1024,2048]{1,0:T(8,128)} fusion(bf16[1024,2048]{0,1:T(8,128)(2,1)} %all-gather.16.cloned.1.call-done, bf16[512,1024]{1,0:T(8,128)(2,1)} %collective-permute-done, bf16[512,1024]{1,0:T(8,128)(2,1)S(1)} %add_convert_fusion.1), kind=kOutput, calls=%fused_computation.139 | convolution fusion | flops 4299161600 | bytes 14680064 | tf_op jit(solution)/shard_map/dot_general | solution.py:203
  291.1 31.1 %all-gather.20.cloned.1.call-done = bf16[1024,2048]{0,1:T(8,128)(2,1)} async-done(((bf16[256,2048]{0,1:T(8,128)(2,1)}), bf16[1024,2048]{0,1:T(8,128)(2,1)}) %all-gather.20.cloned.1.call-update) | async-done | bytes 4194320 | tf_op jit(solution)/shard_map/all_gather | solution.py:160
  322.1 9.0 %fusion.120 = f32[1024,1024]{1,0:T(8,128)S(1)} fusion(bf16[1024,2048]{0,1:T(8,128)(2,1)} %all-gather.20.cloned.1.call-done, f32[1024,2048]{1,0:T(8,128)} %fusion.85), kind=kOutput, calls=%fused_computation.219 | convolution fusion | flops 4313841664 | bytes 16777216 | tf_op jit(solution)/shard_map/dot_general | solution.py:126
  340.7 11.2 %fusion.10 = bf16[1024,2048]{1,0:T(8,128)(2,1)} fusion(f32[1024,2048]{1,0:T(8,128)S(1)} %copy-done.73, bf16[1024,2048]{0,1:T(8,128)(2,1)S(1)} %copy-done.70, bf16[512,1024]{1,0:T(8,128)(2,1)S(1)} %collective-permute-done.4, bf16[512,1024]{1,0:T(8,128)(2,1)S(1)} %get-tuple-element.197), kind=kOutput, calls=%fused_computation.24 | convolution fusion | flops 4341104640 | bytes 18874368 | tf_op jit(solution)/shard_map/dot_general | solution.py:214
  370.8 10.3 %convolution_convert_fusion.1 = bf16[1024,2048]{1,0:T(8,128)(2,1)} fusion(bf16[512,1024]{1,0:T(8,128)(2,1)S(1)} %copy-done.72, bf16[512,1024]{1,0:T(8,128)(2,1)S(1)} %get-tuple-element.197, f32[1024,2048]{1,0:T(8,128)} %fusion.85), kind=kOutput, calls=%fused_computation.51 | convolution fusion | flops 4320133120 | bytes 14680064 | tf_op jit(solution)/shard_map/dot_general | solution.py:120
  391.4 9.2 %convolution_convert_fusion.2 = bf16[1024,2048]{1,0:T(8,128)(2,1)} fusion(bf16[1024,2048]{1,0:T(8,128)(2,1)} %fusion.10, bf16[512,1024]{1,0:T(8,128)(2,1)} %collective-permute-done, bf16[512,1024]{1,0:T(8,128)(2,1)S(1)} %copy-done.51), kind=kOutput, calls=%fused_computation.52 | convolution fusion | flops 4301258752 | bytes 10485760 | tf_op jit(solution)/shard_map/dot_general | solution.py:120
  400.7 16.4 %all-to-all-done.1 = bf16[4,512,256]{2,1,0:T(8,128)(2,1)S(1)} async-done(((bf16[4,512,256]{2,1,0:T(8,128)(2,1)}), bf16[4,512,256]{2,1,0:T(8,128)(2,1)S(1)}, u32[]{:S(2)}, u32[]{:S(2)}) %all-to-all-start.1) | async-done | bytes 1048608 | tf_op jit(solution)/shard_map/all_to_all | solution.py:226
  431.9 8.2 %multiply_reduce_fusion.2 = (f32[4,512]{1,0:T(4,128)S(1)}, f32[4,512,1024]{2,1,0:T(8,128)}) fusion(f32[4,512,1024]{2,1,0:T(8,128)} %copy-done.1, f32[4,512]{1,0:T(4,128)S(1)} %log_add_fusion.2, bf16[512,4,64]{0,2,1:T(8,128)(2,1)S(1)} %bitcast.237, bf16[1024,4,64]{0,2,1:T(8,128)(2,1)S(1)} %bitcast.246), kind=kOutput, calls=%fused_computation.28 | convolution fusion | flops 274724864 | bytes 17580032 | tf_op jit(solution)/shard_map/qgd,kgd->gqk/dot_general | solution.py:93
  455.3 9.8 %multiply_convert_fusion.1 = bf16[4,512,1536]{2,1,0:T(8,128)(2,1)S(1)} fusion(f32[4,512,1536]{2,1,0:T(8,128)} %get-tuple-element.237, f32[4,512,1536]{2,1,0:T(8,128)} %copy-done, f32[4,512]{1,0:T(4,128)S(1)} %get-tuple-element.236, f32[4,512]{1,0:T(4,128)S(1)} %log_add_fusion.1), kind=kLoop, calls=%fused_computation.8 | loop fusion | flops 12582912 | bytes 31473664 | tf_op jit(solution)/shard_map/convert_element_type | solution.py:97
  471.6 9.1 %multiply_reduce_fusion = (f32[4,512]{1,0:T(4,128)S(1)}, f32[4,512,2048]{2,1,0:T(8,128)}) fusion(f32[4,512,2048]{2,1,0:T(8,128)S(1)} %bitcast.204, f32[4,512]{1,0:T(4,128)S(1)} %log_add_fusion, bf16[512,4,64]{0,2,1:T(8,128)(2,1)} %bitcast.225, bf16[2048,4,64]{0,2,1:T(8,128)(2,1)S(1)} %bitcast.216), kind=kOutput, calls=%fused_computation.1 | convolution fusion | flops 549451776 | bytes 34881536 | tf_op jit(solution)/shard_map/qgd,kgd->gqk/dot_general | solution.py:93
  480.8 10.4 %multiply_convert_fusion = bf16[4,512,2048]{2,1,0:T(8,128)(2,1)} fusion(f32[4,512,2048]{2,1,0:T(8,128)} %get-tuple-element.239, f32[4,512,2048]{2,1,0:T(8,128)S(1)} %bitcast.204, f32[4,512]{1,0:T(4,128)S(1)} %get-tuple-element.238, f32[4,512]{1,0:T(4,128)S(1)} %log_add_fusion), kind=kLoop, calls=%fused_computation | loop fusion | flops 16777216 | bytes 41959424 | tf_op jit(solution)/shard_map/convert_element_type | solution.py:97
  535.7 8.3 %fusion.53 = bf16[2048,4,64]{0,2,1:T(8,128)(2,1)S(1)} fusion(f32[2048,4,64]{0,2,1:T(8,128)} %fusion.47, bf16[512,4,64]{0,2,1:T(8,128)(2,1)S(1)} %bitcast.226, f32[4,512,2048]{2,1,0:T(8,128)} %get-tuple-element.223, f32[4,512]{1,0:T(4,128)S(1)} %log_add_fusion), kind=kOutput, calls=%fused_computation.86 | convolution fusion | flops 546308096 | bytes 20193280 | tf_op jit(solution)/shard_map/gqk,qgd->kgd/dot_general | solution.py:91
  557.3 15.8 %reduce-scatter.23.cloned.1.call-done = bf16[1,256,512]{2,1,0:T(8,128)(2,1)} async-done(((bf16[4,256,512]{2,1,0:T(8,128)(2,1)}), bf16[1,256,512]{2,1,0:T(8,128)(2,1)}) %reduce-scatter.23.cloned.1.call-update) | async-done | bytes 262160 | tf_op jit(solution)/shard_map/reduce_scatter | solution.py:166
  574.2 27.0 %reduce-scatter.19.cloned.1.call-done = bf16[1,256,512]{2,1,0:T(8,128)(2,1)} async-done(((bf16[4,256,512]{2,1,0:T(8,128)(2,1)}), bf16[1,256,512]{2,1,0:T(8,128)(2,1)}) %reduce-scatter.19.cloned.1.call-update) | async-done | bytes 262160 | tf_op jit(solution)/shard_map/reduce_scatter | solution.py:166
  602.9 38.3 %reduce-scatter.11.cloned.1.call-done = bf16[128,768]{1,0:T(8,128)(2,1)} async-done(((bf16[1024,768]{1,0:T(8,128)(2,1)}), bf16[128,768]{1,0:T(8,128)(2,1)}) %reduce-scatter.11.cloned.1.call-update) | async-done | bytes 196624 | tf_op jit(solution)/shard_map/reduce_scatter | solution.py:239
  648.6 71.6 %reduce-scatter.9.cloned.1.call-done = bf16[512,1024]{1,0:T(8,128)(2,1)} async-done(((bf16[2048,1024]{1,0:T(8,128)(2,1)}), bf16[512,1024]{1,0:T(8,128)(2,1)}) %reduce-scatter.9.cloned.1.call-update) | async-done | bytes 1048592 | tf_op jit(solution)/shard_map/reduce_scatter | solution.py:237
  723.9 41.5 %all-reduce.2 = (f32[4,1024]{1,0:T(4,128)}, f32[4,1024]{1,0:T(4,128)}) all-reduce(f32[4,1024]{1,0:T(4,128)S(1)} %pad_maximum_fusion.14, f32[4,1024]{1,0:T(4,128)S(1)} %pad_maximum_fusion.15), channel_id=1, replica_groups=mesh['outer'=4,'pair'=2,'head'=4] {'outer','pair','head'}, use_global_device_ids=true, to_apply=%region_40.41 | all-reduce | flops 8192 | bytes 65536 | tf_op jit(solution)/shard_map/psum | solution.py:242
  (346 shorter events, 230.7 us)
Async XLA Ops:
  7.2 38.8 %all-gather.14.cloned.1.call-start = ((), (), s32[]{:S(2)}) async-start(), calls=%async_computation.13 | async-start | bytes 1310720 | tf_op jit(solution)/shard_map/all_gather | solution.py:158
  8.3 1.5 collective-permute-start.1
  10.7 64.5 %all-gather.18.cloned.1.call-start = ((), (), s32[]{:S(2)}) async-start(), calls=%async_computation.15 | async-start | bytes 1310720 | tf_op jit(solution)/shard_map/all_gather | solution.py:158
  14.0 88.0 %all-gather.10.cloned.1.call-start = ((), (), s32[]{:S(2)}) async-start(), calls=%async_computation.11 | async-start | bytes 1769472 | tf_op jit(solution)/shard_map/all_gather | solution.py:178
  15.7 169.1 %all-gather.8.cloned.1.call-start = ((), (), s32[]{:S(2)}) async-start(), calls=%async_computation.10 | async-start | bytes 5242880 | tf_op jit(solution)/shard_map/all_gather | solution.py:183
  17.9 228.9 %all-gather.12.cloned.1.call-start = ((), (), s32[]{:S(2)}) async-start(), calls=%async_computation.12 | async-start | bytes 2359296 | tf_op jit(solution)/shard_map/all_gather | solution.py:184
  36.7 241.3 %all-gather.16.cloned.1.call-start = ((), (), s32[]{:S(2)}) async-start(), calls=%async_computation.14 | async-start | bytes 5242880 | tf_op jit(solution)/shard_map/all_gather | solution.py:160
  48.4 273.8 %all-gather.20.cloned.1.call-start = ((), (), s32[]{:S(2)}) async-start(), calls=%async_computation.16 | async-start | bytes 5242880 | tf_op jit(solution)/shard_map/all_gather | solution.py:160
  243.3 29.4 %all-to-all-start = ((bf16[4,512,256]{1,2,0:T(8,128)(2,1)}), bf16[4,512,256]{1,2,0:T(8,128)(2,1)S(1)}, u32[]{:S(2)}, u32[]{:S(2)}) async-start(bf16[4,512,256]{1,2,0:T(8,128)(2,1)} %copy.76), calls=%async_computation | async-start | bytes 2097152 | tf_op jit(solution)/shard_map/all_to_all | solution.py:193
  246.8 251.5 %reduce-scatter.13.cloned.1.call-start = ((), (), s32[]{:S(2)}) async-start(), calls=%async_computation.19 | async-start | bytes 2359296 | tf_op jit(solution)/shard_map/reduce_scatter | solution.py:229
  277.9 2.9 collective-permute-start
  331.3 2.7 collective-permute-start.3
  338.1 2.7 collective-permute-start.4
  358.4 2.7 collective-permute-start.5
  370.8 138.0 %reduce-scatter.21.cloned.1.call-start = ((), (), s32[]{:S(2)}) async-start(), calls=%async_computation.23 | async-start | bytes 5242880 | tf_op jit(solution)/shard_map/reduce_scatter | solution.py:164
  386.4 30.6 %all-to-all-start.1 = ((bf16[4,512,256]{2,1,0:T(8,128)(2,1)}), bf16[4,512,256]{2,1,0:T(8,128)(2,1)S(1)}, u32[]{:S(2)}, u32[]{:S(2)}) async-start(bf16[4,512,256]{2,1,0:T(8,128)(2,1)} %bitcast.202), calls=%async_computation.1 | async-start | bytes 2097152 | tf_op jit(solution)/shard_map/all_to_all | solution.py:226
  391.0 142.4 %reduce-scatter.17.cloned.1.call-start = ((), (), s32[]{:S(2)}) async-start(), calls=%async_computation.21 | async-start | bytes 5242880 | tf_op jit(solution)/shard_map/reduce_scatter | solution.py:164
  400.6 155.0 %reduce-scatter.15.cloned.1.call-start = ((), (), s32[]{:S(2)}) async-start(), calls=%async_computation.20 | async-start | bytes 327680 | tf_op jit(solution)/shard_map/reduce_scatter | solution.py:231
  500.1 73.0 %reduce-scatter.23.cloned.1.call-start = ((), (), s32[]{:S(2)}) async-start(), calls=%async_computation.24 | async-start | bytes 1310720 | tf_op jit(solution)/shard_map/reduce_scatter | solution.py:166
  511.3 90.0 %reduce-scatter.19.cloned.1.call-start = ((), (), s32[]{:S(2)}) async-start(), calls=%async_computation.22 | async-start | bytes 1310720 | tf_op jit(solution)/shard_map/reduce_scatter | solution.py:166
  535.6 105.6 %reduce-scatter.11.cloned.1.call-start = ((), (), s32[]{:S(2)}) async-start(), calls=%async_computation.18 | async-start | bytes 1769472 | tf_op jit(solution)/shard_map/reduce_scatter | solution.py:239
  548.8 171.4 %reduce-scatter.9.cloned.1.call-start = ((), (), s32[]{:S(2)}) async-start(), calls=%async_computation.17 | async-start | bytes 5242880 | tf_op jit(solution)/shard_map/reduce_scatter | solution.py:237
  574.1 68.8 %collective-permute-start.7 = (bf16[128,512]{1,0:T(8,128)(2,1)S(1)}, bf16[128,512]{1,0:T(8,128)(2,1)}, u32[]{:S(2)}, u32[]{:S(2)}) collective-permute-start(bf16[128,512]{1,0:T(8,128)(2,1)S(1)} %get-tuple-element.204), channel_id=1, source_target_pairs={{0,4},{4,0},{1,5},{5,1},{2,6},{6,2},{3,7},{7,3},{8,12},{12,8},{9,1... | collective-permute-start | bytes 393224 | tf_op jit(solution)/shard_map/ppermute | solution.py:135
  602.9 43.9 %collective-permute-start.6 = (bf16[128,512]{1,0:T(8,128)(2,1)}, bf16[128,512]{1,0:T(8,128)(2,1)}, u32[]{:S(2)}, u32[]{:S(2)}) collective-permute-start(bf16[128,512]{1,0:T(8,128)(2,1)} %get-tuple-element.206), channel_id=1, source_target_pairs={{0,4},{4,0},{1,5},{5,1},{2,6},{6,2},{3,7},{7,3},{8,12},{12,8},{9,1... | collective-permute-start | bytes 393224 | tf_op jit(solution)/shard_map/ppermute | solution.py:135
  (87 other events, 1522.5 us)
Sparse Core Ops, SparseCore 0:
  10.8 35.2 all-gather.13
  48.2 26.8 all-gather.17
  77.0 24.9 all-gather.9
  104.0 80.7 all-gather.7
  186.5 26.5 all-gather.11
  214.8 52.4 all-gather.15
  269.7 52.4 all-gather.19
  370.9 41.0 reduce-scatter.12
  415.0 52.5 reduce-scatter.20
  470.4 52.5 reduce-scatter.16
  525.3 19.9 reduce-scatter.14
  547.5 25.5 reduce-scatter.22
  575.4 25.7 reduce-scatter.18
  604.4 36.7 reduce-scatter.10
  643.4 76.7 reduce-scatter.8

commit v2 on v1

--- a/solution.py
+++ b/solution.py
@@ -127,12 +127,27 @@
         left_op, right_op, (((1,), (1,)), ((), ())), preferred_element_type=jnp.float32
     )
 
+
 WIDE = ("outer", "pair")
 ALL = ("outer", "pair", "head")
+LINE = ("pair", "head")
+HEADS = 4
 
 
 def swap(values):
     return lax.ppermute(values, "pair", [(0, 1), (1, 0)])
+
+
+def send(values, moves):
+    return lax.ppermute(values, LINE, [(a * HEADS + b, c * HEADS + d) for (a, b), (c, d) in moves])
+
+
+def both(moves):
+    return [((p, a), (p, b)) for p in range(2) for a, b in moves]
+
+
+def shift(values, step):
+    return lax.ppermute(values, "head", [(i, (i + step) % HEADS) for i in range(HEADS)])
 
 
 def halves(block, axis):
@@ -152,113 +167,262 @@
     )
 
 
-def gather_half(block):
+def after(values, earlier):
+    return lax.optimization_barrier((values, earlier))[0]
+
+
+def spread(block, axis):
+    return jnp.concatenate([block] + [shift(block, k) for k in range(1, HEADS)], axis=axis)
+
+
+def collect(blocks):
+    total = blocks[0].astype(jnp.float32)
+    for k in range(1, HEADS):
+        total = total + shift(blocks[k], -k).astype(jnp.float32)
+    return total
+
+
+def half_rows(block):
     own, other = halves(block, 1)
-    pair_rows = in_order(own, swap(other), 0)
-    columns = lax.all_gather(pair_rows, "head", axis=0, tiled=False)
-    columns = columns.transpose(1, 0, 2).reshape(pair_rows.shape[0], -1)
-    return lax.all_gather(columns, "outer", axis=0, tiled=True)
-
-
-def scatter_half(grad, groups):
+    return in_order(own, swap(other), 0)
+
+
+def scatter_half(grad):
     rows = lax.psum_scatter(grad, "outer", scatter_dimension=0, tiled=True)
-    blocks = rows.reshape(rows.shape[0], groups, -1).transpose(1, 0, 2)
-    block = lax.psum_scatter(blocks, "head", scatter_dimension=0, tiled=False)
+    block = collect(jnp.split(rows, HEADS, axis=1)).astype(jnp.bfloat16)
     own, other = halves(block, 0)
-    return in_order(own, swap(other), 1)
+    return in_order(own, swap(other), 1).astype(jnp.float32)
+
+
+FORWARD = [((z // 2, z), (1 - z // 2, z)) for z in range(HEADS)]
+
+
+def sequence_rows(block):
+    place = lax.axis_index("head")
+    holds = lax.axis_index("pair") == place // 2
+    inner = (place == 1) | (place == 2)
+    near = send(
+        block,
+        [((0, 0), (0, 1)), ((0, 1), (0, 0)), ((1, 2), (1, 3)), ((1, 3), (1, 2))],
+    )
+    next_in = send(block, [((0, 2), (0, 1)), ((1, 1), (1, 2))])
+    last_in = send(block, [((0, 3), (0, 1)), ((1, 0), (1, 2))])
+    outward = [((0, 1), (0, 0)), ((1, 2), (1, 3))]
+    next_out = send(next_in, outward)
+    last_out = send(last_in, outward)
+    pieces = (
+        block,
+        near,
+        jnp.where(inner, next_in, next_out),
+        jnp.where(inner, last_in, last_out),
+    )
+    own, near, following, last = (jnp.where(holds, v, send(v, FORWARD)) for v in pieces)
+    first = jnp.where(place % 2 == 0, own, near)
+    second = jnp.where(place % 2 == 0, near, own)
+    low = place < 2
+    return jnp.concatenate(
+        [
+            jnp.where(low, first, last),
+            jnp.where(low, second, following),
+            jnp.where(low, following, first),
+            jnp.where(low, last, second),
+        ],
+        axis=0,
+    )
+
+
+def sequence_sum(partial):
+    place = lax.axis_index("head")
+    pair = lax.axis_index("pair")
+    low = place < 2
+    inner = (place == 1) | (place == 2)
+    own, other = halves(partial, 1)
+    half = own.astype(jnp.float32) + swap(other).astype(jnp.float32)
+    rows = half.shape[0] // HEADS
+
+    def block(i):
+        index = jnp.where(low, i, HEADS - 1 - i)
+        return lax.dynamic_slice_in_dim(half, index * rows, rows, 0)
+
+    inward = both([(0, 1), (3, 2)])
+    near_moves = both([(0, 1), (1, 0), (2, 3), (3, 2)])
+    bf16 = jnp.bfloat16
+    last = block(3) + send(block(3).astype(bf16), inward).astype(jnp.float32)
+    last = send(last.astype(bf16), both([(1, 3), (2, 0)]))
+    following = block(2) + send(block(2).astype(bf16), inward).astype(jnp.float32)
+    following = send(following.astype(bf16), both([(1, 2), (2, 1)]))
+    away = jnp.where(inner, block(0), block(1)).astype(bf16)
+    mine = jnp.where(inner, block(1), block(0)) + send(away, near_moves).astype(jnp.float32)
+    far = jnp.where(inner, following, last).astype(jnp.float32)
+    keeps = pair == place // 2
+    kept = jnp.where(keeps, mine, far)
+    given = swap(jnp.where(keeps, far, mine).astype(bf16)).astype(jnp.float32)
+    return in_order(kept, given, 1)
+
+
+def group_moves(k):
+    moves = []
+    for p in range(2):
+        for z in range(HEADS):
+            group = 2 * (z % 2) + p
+            moves.append(((p, z), (z // 2, (group + k) % HEADS)))
+    return moves
+
+
+def column_moves(k):
+    moves = []
+    for p in range(2):
+        for group in range(HEADS):
+            moves.append(((p, group), (group % 2, group // 2 + 2 * (p ^ k))))
+    return moves
+
+
+def turned(moves):
+    return [(b, a) for a, b in moves]
+
+
+def group_to_rows(values):
+    rows = values.shape[0] // HEADS
+    group = 2 * (lax.axis_index("head") % 2) + lax.axis_index("pair")
+    parts = []
+    for k in range(HEADS):
+        start = (group + k) % HEADS * rows
+        parts.append(send(lax.dynamic_slice_in_dim(values, start, rows, 0), group_moves(k)))
+    return jnp.concatenate(parts, axis=1)
+
+
+def rows_to_group(values):
+    group = 2 * (lax.axis_index("head") % 2) + lax.axis_index("pair")
+    rows = values.shape[0]
+    parts = [
+        send(part, turned(group_moves(k)))
+        for k, part in enumerate(jnp.split(values, HEADS, axis=1))
+    ]
+    twice = jnp.concatenate(parts + parts, axis=0)
+    start = (HEADS - group) % HEADS * rows
+    return lax.dynamic_slice_in_dim(twice, start, HEADS * rows, 0)
+
+
+def sum_all(values):
+    for axis in ALL:
+        size = lax.axis_size(axis)
+        step = 1
+        while step < size:
+            values = values + lax.ppermute(values, axis, [(i, i ^ step) for i in range(size)])
+            step *= 2
+    return values
 
 
 def on_device(
     tokens, cotangent, w_query, w_key, w_value, w_out, w_up, w_down, norm_gain, norm_bias
 ):
-    groups = lax.axis_size("head")
     rows = tokens.shape[0]
     width = w_query.shape[1]
+    model = w_query.shape[0] * lax.axis_size("outer") * 2
     bf16 = jnp.bfloat16
-    w_attn = lax.all_gather(
-        jnp.concatenate([w_query, w_key, w_value], axis=1), WIDE, axis=0, tiled=True
-    )
-    residual = tokens.astype(jnp.float32)
+    f32 = jnp.float32
+    late = lax.axis_index("head") // 2
+    residual = tokens.astype(f32)
     norm_a, unit_a, inv_a = normalize(residual, norm_gain[0], norm_bias[0])
-    seq_a = lax.all_gather(norm_a.astype(bf16), "head", axis=0, tiled=True)
-    full_o = lax.all_gather(
-        lax.all_gather(w_out, "head", axis=0, tiled=True).T, WIDE, axis=0, tiled=True
-    )
-    full_up = gather_half(w_up)
-    full_down = gather_half(w_down.T)
+
+    w_cols = jnp.concatenate([w_query, w_key, w_value], axis=1)
+    w_first, w_second = (send(w_cols, column_moves(k)) for k in range(2))
+    w_cols = jnp.where(
+        late == 0,
+        jnp.concatenate([w_first, w_second], axis=0),
+        jnp.concatenate([w_second, w_first], axis=0),
+    )
+    w_cols = lax.all_gather(w_cols, "outer", axis=0, tiled=True)
+    seq_a = sequence_rows(norm_a.astype(bf16))
+    out_rows = spread(w_out.T, 1)
+    out_own = lax.all_gather(out_rows, "outer", axis=0, tiled=False)
+    full_up = lax.all_gather(spread(half_rows(w_up), 1), "outer", axis=0, tiled=True)
+    full_down = lax.all_gather(spread(half_rows(w_down.T), 1), "outer", axis=0, tiled=True)
+
     block_rows = min(512, seq_a.shape[0])
-    qkv = jnp.dot(seq_a, w_attn, preferred_element_type=jnp.float32).astype(bf16)
+    qkv = jnp.dot(seq_a, w_cols, preferred_element_type=f32).astype(bf16)
     queries, key_rows, value_rows = (qkv[:, i * width : (i + 1) * width] for i in range(3))
     attended, totals = attend(queries, key_rows, value_rows, block_rows)
-    attended = lax.all_to_all(
-        attended.astype(bf16).reshape(groups, rows, width), "head", 0, 0, tiled=False
-    )
-    attended = attended.transpose(1, 0, 2).reshape(rows, groups * width)
+    attended = group_to_rows(attended.astype(bf16))
+    out_other = swap(out_own)
+    place = lax.axis_index("pair")
+    full_o = jnp.stack(
+        [jnp.where(place == 0, out_own, out_other), jnp.where(place == 0, out_other, out_own)],
+        axis=1,
+    ).reshape(model, -1)
     mixed = contract_cols(attended, full_o)
     norm_z, unit_z, inv_z = normalize(mixed, norm_gain[1], norm_bias[1])
     hidden = residual + norm_z
     norm_c, unit_c, inv_c = normalize(hidden, norm_gain[2], norm_bias[2])
     rows_c = norm_c.astype(bf16)
     pair_c = jnp.concatenate([rows_c, swap(rows_c)], axis=0)
-    pre_act = jnp.dot(pair_c, full_up, preferred_element_type=jnp.float32)
+    pre_act = jnp.dot(pair_c, full_up, preferred_element_type=f32)
     active, gelu_back = jax.vjp(jax.nn.gelu, pre_act)
     active = active.astype(bf16)
-    both = contract_cols(active, full_down)
-    output = both[:rows] + swap(both[rows:].astype(bf16)).astype(jnp.float32)
+    both_m = contract_cols(active, full_down)
+    output = both_m[:rows] + swap(both_m[rows:].astype(bf16)).astype(f32)
     norm_m, unit_m, inv_m = normalize(output, norm_gain[3], norm_bias[3])
     block_out = (hidden + norm_m).astype(bf16)
-    grad_y = cotangent.astype(jnp.float32)
+
+    grad_y = cotangent.astype(f32)
     grad_m, gain_m, bias_m = normalize_back(grad_y, unit_m, inv_m, norm_gain[3])
     rows_gm = grad_m.astype(bf16)
     pair_gm = jnp.concatenate([rows_gm, swap(rows_gm)], axis=0)
-    grad_act = jnp.dot(pair_gm, full_down, preferred_element_type=jnp.float32)
+    grad_act = jnp.dot(pair_gm, full_down, preferred_element_type=f32)
     grad_pre = gelu_back(grad_act)[0].astype(bf16)
     both_c = contract_cols(grad_pre, full_up)
-    grad_c = both_c[:rows] + swap(both_c[rows:].astype(bf16)).astype(jnp.float32)
-    grad_down = scatter_half(contract_rows(pair_gm, active).astype(bf16), groups).T
-    grad_up = scatter_half(contract_rows(pair_c, grad_pre).astype(bf16), groups)
+    grad_c = both_c[:rows] + swap(both_c[rows:].astype(bf16)).astype(f32)
+    grad_down = scatter_half(contract_rows(pair_gm, active).astype(bf16)).T
+    grad_up = scatter_half(contract_rows(pair_c, grad_pre).astype(bf16))
     grad_more, gain_c, bias_c = normalize_back(grad_c, unit_c, inv_c, norm_gain[2])
     grad_h = grad_y + grad_more
     grad_z, gain_z, bias_z = normalize_back(grad_h, unit_z, inv_z, norm_gain[1])
     rows_gz = grad_z.astype(bf16)
-    grad_att = jnp.dot(rows_gz, full_o, preferred_element_type=jnp.float32).astype(bf16)
-    grad_att = grad_att.reshape(rows, groups, width).transpose(1, 0, 2)
-    grad_att = lax.all_to_all(grad_att, "head", 0, 0, tiled=False)
-    grad_att = grad_att.reshape(groups * rows, width)
+    grad_att = jnp.dot(rows_gz, full_o, preferred_element_type=f32).astype(bf16)
+    grad_att = rows_to_group(grad_att)
     grad_o = contract_rows(rows_gz, attended).astype(bf16)
-    grad_o = lax.psum_scatter(grad_o, WIDE, scatter_dimension=0, tiled=True)
-    grad_o = grad_o.T.reshape(groups, width, -1)
-    grad_o = lax.psum_scatter(grad_o, "head", scatter_dimension=0, tiled=False)
+    grad_o = grad_o.reshape(-1, 2, w_out.shape[1], attended.shape[1])
+    own_o, other_o = halves(grad_o, 1)
+    grad_o = (own_o.astype(f32) + swap(other_o).astype(f32)).astype(bf16)
+    grad_o = grad_o.reshape(-1, attended.shape[1])
+    grad_o = lax.psum_scatter(grad_o, "outer", scatter_dimension=0, tiled=True)
+    grad_o = collect(jnp.split(grad_o, HEADS, axis=1)).T
     grad_queries, grad_keys, grad_values = attend_back(
         queries, key_rows, value_rows, grad_att, totals, block_rows
     )
     grad_qkv = jnp.concatenate([grad_queries, grad_keys, grad_values], axis=1)
-    grad_a = contract_cols(grad_qkv, w_attn).astype(bf16)
-    grad_a = lax.psum_scatter(grad_a, "head", scatter_dimension=0, tiled=True).astype(jnp.float32)
+    grad_a = sequence_sum(contract_cols(grad_qkv, w_cols).astype(bf16))
     grad_w = contract_rows(seq_a, grad_qkv).astype(bf16)
-    grad_w = lax.psum_scatter(grad_w, WIDE, scatter_dimension=0, tiled=True).astype(jnp.float32)
+    grad_w = lax.psum_scatter(grad_w, "outer", scatter_dimension=0, tiled=True)
+    size = grad_w.shape[0] // 2
+    parts = [
+        send(
+            lax.dynamic_slice_in_dim(grad_w, jnp.where(late == k, 0, size), size, 0),
+            turned(column_moves(k)),
+        ).astype(f32)
+        for k in range(2)
+    ]
+    grad_w = parts[0] + parts[1]
     grad_first, gain_a, bias_a = normalize_back(grad_a, unit_a, inv_a, norm_gain[0])
     input_grad = grad_h + grad_first
-    gain_grad, bias_grad = lax.psum(
-        (jnp.stack([gain_a, gain_z, gain_c, gain_m]), jnp.stack([bias_a, bias_z, bias_c, bias_m])),
-        ALL,
-    )
+    sums = sum_all(jnp.stack([gain_a, gain_z, gain_c, gain_m, bias_a, bias_z, bias_c, bias_m]))
     return (
         block_out,
         input_grad,
         grad_w[:, :width],
         grad_w[:, width : 2 * width],
         grad_w[:, 2 * width :],
-        grad_o.astype(jnp.float32),
-        grad_up.astype(jnp.float32),
-        grad_down.astype(jnp.float32),
-        gain_grad,
-        bias_grad,
+        grad_o,
+        grad_up,
+        grad_down,
+        sums[:4],
+        sums[4:],
     )
 
 
 def solution(mesh):
     wide, head = mesh.shape["wide"], mesh.shape["head"]
+    assert head == HEADS and wide % 2 == 0
     paired = Mesh(mesh.devices.reshape(wide // 2, 2, head), ALL)
     rows = P(ALL, None)
     by_rows = P(WIDE, "head")

time: 779 us -> 650 us (0.83)
  waiting for transfers between devices: 378 us -> 206 us
  starting transfers between devices: 11.2 us -> 99.3 us
  blocking collectives: 60.2 us -> 0 us
  other arithmetic: 73 us -> 99.5 us
  matrix products: 190 us -> 173 us
    ppermute x0 -> x49, waiting for transfers between devices: none -> 172 us  [the longest x26 96.3 us: send(): lax.ppermute(values, LINE, [(a * HEADS + b, c * HEADS + d) for (a, b), (c...]
    all_gather x7 -> x4, waiting for transfers between devices: 170 us -> 0.02 us  [the longest x1 0.02 us: on_device(): out_own = lax.all_gather(out_rows, 'outer', axis=0, tiled=False)]
    reduce_scatter x6 -> x1, waiting for transfers between devices: 153 us -> 0.01 us  [on_device(): grad_w = lax.psum_scatter(grad_w, 'outer', scatter_dimension=0, tiled=True)]
    ppermute x0 -> x49, starting transfers between devices: none -> 91.1 us  [the longest x26 51.2 us: send(): lax.ppermute(values, LINE, [(a * HEADS + b, c * HEADS + d) for (a, b), (c...]
    all_to_all x2 -> x0, waiting for transfers between devices: 42.1 us -> none  [the longest x1 25.8 us: on_device(): lax.all_to_all(attended.astype(bf16).reshape(groups, rows, width), 'head'...]
    psum x1 -> x0, blocking collectives: 41.5 us -> none  [on_device(): lax.psum((jnp.stack([gain_a, gain_z, gain_c, gain_m]), jnp.stack([bias_a,...]
    reduce_scatter x2, waiting for transfers between devices: 0.02 us -> 19.6 us  [scatter_half(): rows = lax.psum_scatter(grad, 'outer', scatter_dimension=0, tiled=True)]
    all_gather x1 -> x0, blocking collectives: 18.6 us -> none  [on_device(): lax.all_gather(w_out, 'head', axis=0, tiled=True)]
  transfers between devices with their start and end apart: 25 -> 69, of which waited for: 17 -> 33; matrix products, arithmetic and copies ran while one was open for 32% -> 40% of each run, Pallas kernels for 0% -> 0%
where the time goes in v2:
time: 650 us; the launch traced here: 644 us
  waiting for transfers between devices  206 us (32%)
  matrix products  173 us (27%)
  other arithmetic  99.5 us (15%)
  starting transfers between devices  99.3 us (15%)
  local copies, waits for them, and re-layouts  49.9 us (8%)
  between operations  16.1 us (2%)
    ppermute x26, waiting for transfers between devices, send(): lax.ppermute(values, LINE, [(a * HEADS + b, c * HEADS + d) for (a, b), (c...  96.3 us
    ppermute x18, waiting for transfers between devices, shift(): lax.ppermute(values, 'head', [(i, (i + step) % HEADS) for i in range(HEAD...  70.2 us
    ppermute x26, starting transfers between devices, send(): lax.ppermute(values, LINE, [(a * HEADS + b, c * HEADS + d) for (a, b), (c...  51.2 us
    ppermute x18, starting transfers between devices, shift(): lax.ppermute(values, 'head', [(i, (i + step) % HEADS) for i in range(HEAD...  33.7 us
    dot_general x4, matrix products, contract_rows(): lax.dot_general(left_op, right_op, (((0,), (0,)), ((), ())), preferred_el...  25.3 us
    convert_element_type x4, other arithmetic, attend_back(): grad_scores = (weights * (grad_weights - inner_sum)).astype(jnp.bfloat16)  25.2 us
    unnamed x237, local copies, waits for them, and re-layouts  24.3 us
    dot_general x4, matrix products, attend_back(): jnp.einsum('gqk,qgd->kgd', rounded, grad_block, preferred_element_type=jn...  22.6 us
  transfers between devices with their start and end apart: 69, of which 33 were waited for; matrix products, arithmetic and copies ran while one was open for 40% of the time, Pallas kernels for 0%

profile of v2, /device:TPU:0, one launch (start us, length us, event | category | flops | bytes accessed | tf_op | source)
XLA Modules:
  0.0 643.7 jit_solution(15421576536900737646)
XLA Ops:
  44.9 18.1 %collective-permute-done.22 = bf16[256,512]{0,1:T(8,128)(2,1)S(1)} collective-permute-done((bf16[256,512]{0,1:T(8,128)(2,1)S(1)}, bf16[256,512]{0,1:T(8,128)(2,1)S(1)}, u32[]{:S(2)}, u32[]{:S(2)}) %collective-permute-start.22) | collective-permute-done | bytes 262176 | tf_op jit(solution)/shard_map/ppermute | solution.py:150
  80.6 11.5 %collective-permute-done.1 = bf16[512,1024]{1,0:T(8,128)(2,1)} collective-permute-done((bf16[512,1024]{1,0:T(8,128)(2,1)}, bf16[512,1024]{1,0:T(8,128)(2,1)}, u32[]{:S(2)}, u32[]{:S(2)}) %collective-permute-start.1) | collective-permute-done | bytes 1048608 | tf_op jit(solution)/shard_map/ppermute | solution.py:142
  97.1 10.8 %collective-permute-done.4 = bf16[512,1024]{1,0:T(8,128)(2,1)} collective-permute-done((bf16[512,1024]{1,0:T(8,128)(2,1)S(1)}, bf16[512,1024]{1,0:T(8,128)(2,1)}, u32[]{:S(2)}, u32[]{:S(2)}) %collective-permute-start.4) | collective-permute-done | bytes 1048608 | tf_op jit(solution)/shard_map/ppermute | solution.py:142
  122.5 17.5 %collective-permute-done.26 = bf16[256,512]{0,1:T(8,128)(2,1)S(1)} collective-permute-done((bf16[256,512]{0,1:T(8,128)(2,1)S(1)}, bf16[256,512]{0,1:T(8,128)(2,1)S(1)}, u32[]{:S(2)}, u32[]{:S(2)}) %collective-permute-start.26) | collective-permute-done | bytes 262176 | tf_op jit(solution)/shard_map/ppermute | solution.py:150
  185.5 7.5 %fusion.137 = (f32[4,512]{1,0:T(4,128)S(1)}, f32[4,512,2048]{2,1,0:T(8,128)}) fusion(bf16[512,4,64]{0,2,1:T(8,128)(2,1)S(1)} %bitcast.188, bf16[2048,4,64]{0,2,1:T(8,128)(2,1)S(1)} %bitcast.174, pred[512,2048]{1,0:T(8,128)(4,1)S(1)} %iota_compare_fusion), kind=kOutput, calls=%fused_computation.290 | convolution fusion | flops 549451776 | bytes 19144704 | tf_op jit(solution)/shard_map/qgd,kgd->gqk/dot_general | solution.py:34
  193.0 8.2 %fusion = f32[4,512]{1,0:T(4,128)S(1)} fusion(f32[4,512,2048]{2,1,0:T(8,128)} %get-tuple-element.248, f32[4,512]{1,0:T(4,128)S(1)} %get-tuple-element.247), kind=kLoop, calls=%fused_computation.6 | loop fusion | flops 8386560 | bytes 16793600 | tf_op jit(solution)/shard_map/reduce_sum | solution.py:60
  201.2 7.7 %fusion.105 = bf16[512,4,64]{0,2,1:T(8,128)(2,1)S(1)} fusion(bf16[2048,4,64]{0,2,1:T(8,128)(2,1)S(1)} %bitcast.178, f32[4,512,2048]{2,1,0:T(8,128)} %get-tuple-element.248, f32[4,512]{1,0:T(4,128)S(1)} %fusion, f32[4,512]{1,0:T(4,128)S(1)} %get-tuple-element.247), kind=kOutput, calls=%fused_computation.163 | convolution fusion | flops 549584896 | bytes 18104320 | tf_op jit(solution)/shard_map/gqk,kgd->qgd/dot_general | solution.py:63
  225.4 10.2 %collective-permute-done.12 = bf16[512,256]{0,1:T(8,128)(2,1)S(1)} collective-permute-done((bf16[512,256]{0,1:T(8,128)(2,1)S(1)}, bf16[512,256]{0,1:T(8,128)(2,1)S(1)}, u32[]{:S(2)}, u32[]{:S(2)}) %collective-permute-start.12) | collective-permute-done | bytes 262176 | tf_op jit(solution)/shard_map/ppermute | solution.py:142
  243.0 10.3 %fusion.84 = f32[1024,2048]{1,0:T(8,128)} fusion(bf16[1024,2048]{0,1:T(8,128)(2,1)} %all-gather.8.cloned.1.call-done, bf16[512,1024]{1,0:T(8,128)(2,1)} %collective-permute-done.19, bf16[512,1024]{1,0:T(8,128)(2,1)S(1)} %add_convert_fusion.2), kind=kOutput, calls=%fused_computation.141 | convolution fusion | flops 4299161600 | bytes 14680064 | tf_op jit(solution)/shard_map/dot_general | solution.py:359
  253.4 9.2 %fusion.122 = f32[1024,1024]{1,0:T(8,128)S(1)} fusion(bf16[1024,2048]{0,1:T(8,128)(2,1)} %all-gather.10.cloned.1.call-done, f32[1024,2048]{1,0:T(8,128)} %fusion.84), kind=kOutput, calls=%fused_computation.275 | convolution fusion | flops 4313841664 | bytes 16777216 | tf_op jit(solution)/shard_map/dot_general | solution.py:126
  272.2 11.1 %fusion.10 = bf16[1024,2048]{1,0:T(8,128)(2,1)} fusion(f32[1024,2048]{1,0:T(8,128)S(1)} %copy-done.96, bf16[1024,2048]{0,1:T(8,128)(2,1)S(1)} %copy-done.93, bf16[512,1024]{1,0:T(8,128)(2,1)S(1)} %collective-permute-done.29, bf16[512,1024]{1,0:T(8,128)(2,1)S(1)} %get-tuple-element.196), kind=kOutput, calls=%fused_computation.24 | convolution fusion | flops 4341104640 | bytes 18874368 | tf_op jit(solution)/shard_map/dot_general | solution.py:371
  321.6 14.9 %collective-permute-done.33 = bf16[512,256]{1,0:T(8,128)(2,1)S(1)} collective-permute-done((bf16[512,256]{1,0:T(8,128)(2,1)S(1)}, bf16[512,256]{1,0:T(8,128)(2,1)S(1)}, u32[]{:S(2)}, u32[]{:S(2)}) %collective-permute-start.33) | collective-permute-done | bytes 262176 | tf_op jit(solution)/shard_map/ppermute | solution.py:142
  347.2 7.7 %multiply_reduce_fusion.2 = (f32[4,512]{1,0:T(4,128)S(1)}, f32[4,512,1024]{2,1,0:T(8,128)}) fusion(f32[4,512,1024]{2,1,0:T(8,128)} %copy-done.1, f32[4,512]{1,0:T(4,128)S(1)} %log_add_fusion.2, bf16[512,4,64]{0,2,1:T(8,128)(2,1)S(1)} %bitcast.198, bf16[1024,4,64]{0,2,1:T(8,128)(2,1)S(1)} %bitcast.211), kind=kOutput, calls=%fused_computation.28 | convolution fusion | flops 274724864 | bytes 17580032 | tf_op jit(solution)/shard_map/qgd,kgd->gqk/dot_general | solution.py:93
  393.5 7.8 %multiply_reduce_fusion = (f32[4,512]{1,0:T(4,128)S(1)}, f32[4,512,2048]{2,1,0:T(8,128)}) fusion(f32[4,512,2048]{2,1,0:T(8,128)S(1)} %bitcast.167, f32[4,512]{1,0:T(4,128)S(1)} %log_add_fusion, bf16[512,4,64]{0,2,1:T(8,128)(2,1)S(1)} %bitcast.186, bf16[2048,4,64]{0,2,1:T(8,128)(2,1)S(1)} %bitcast.179), kind=kOutput, calls=%fused_computation.1 | convolution fusion | flops 549451776 | bytes 34881536 | tf_op jit(solution)/shard_map/qgd,kgd->gqk/dot_general | solution.py:93
  401.4 11.0 %multiply_convert_fusion = bf16[4,512,2048]{2,1,0:T(8,128)(2,1)} fusion(f32[4,512,2048]{2,1,0:T(8,128)} %get-tuple-element.264, f32[4,512,2048]{2,1,0:T(8,128)S(1)} %bitcast.167, f32[4,512]{1,0:T(4,128)S(1)} %get-tuple-element.263, f32[4,512]{1,0:T(4,128)S(1)} %log_add_fusion), kind=kLoop, calls=%fused_computation | loop fusion | flops 16777216 | bytes 41959424 | tf_op jit(solution)/shard_map/convert_element_type | solution.py:97
  432.9 8.7 %fusion.50 = bf16[2048,4,64]{0,2,1:T(8,128)(2,1)S(1)} fusion(f32[2048,4,64]{0,2,1:T(8,128)} %fusion.44, bf16[512,4,64]{0,2,1:T(8,128)(2,1)S(1)} %bitcast.187, f32[4,512,2048]{2,1,0:T(8,128)} %get-tuple-element.248, f32[4,512]{1,0:T(4,128)S(1)} %log_add_fusion), kind=kOutput, calls=%fused_computation.82 | convolution fusion | flops 546308096 | bytes 20193280 | tf_op jit(solution)/shard_map/gqk,qgd->kgd/dot_general | solution.py:91
  447.4 10.2 %convolution_convert_fusion.1 = bf16[1024,2048]{1,0:T(8,128)(2,1)} fusion(bf16[512,1024]{1,0:T(8,128)(2,1)S(1)} %copy-done.95, bf16[512,1024]{1,0:T(8,128)(2,1)S(1)} %copy-done.54, f32[1024,2048]{1,0:T(8,128)} %fusion.84), kind=kOutput, calls=%fused_computation.53 | convolution fusion | flops 4320133120 | bytes 14680064 | tf_op jit(solution)/shard_map/dot_general | solution.py:120
  458.9 9.1 %convolution_convert_fusion.2 = bf16[1024,2048]{1,0:T(8,128)(2,1)} fusion(bf16[1024,2048]{1,0:T(8,128)(2,1)} %fusion.10, bf16[512,1024]{1,0:T(8,128)(2,1)} %collective-permute-done.19, bf16[512,1024]{1,0:T(8,128)(2,1)S(1)} %copy-done.61), kind=kOutput, calls=%fused_computation.54 | convolution fusion | flops 4301258752 | bytes 10485760 | tf_op jit(solution)/shard_map/dot_general | solution.py:120
  487.2 10.9 %collective-permute-done.39 = bf16[512,512]{1,0:T(8,128)(2,1)S(1)} collective-permute-done((bf16[512,512]{1,0:T(8,128)(2,1)S(1)}, bf16[512,512]{1,0:T(8,128)(2,1)S(1)}, u32[]{:S(2)}, u32[]{:S(2)}) %collective-permute-start.39) | collective-permute-done | bytes 524320 | tf_op jit(solution)/shard_map/ppermute | solution.py:142
  498.1 11.2 %collective-permute-done.37 = bf16[512,512]{1,0:T(8,128)(2,1)S(1)} collective-permute-done((bf16[512,512]{1,0:T(8,128)(2,1)S(1)}, bf16[512,512]{1,0:T(8,128)(2,1)S(1)}, u32[]{:S(2)}, u32[]{:S(2)}) %collective-permute-start.37) | collective-permute-done | bytes 524320 | tf_op jit(solution)/shard_map/ppermute | solution.py:142
  511.7 8.3 %collective-permute-done.36 = bf16[512,512]{1,0:T(8,128)(2,1)S(1)} collective-permute-done((bf16[512,512]{1,0:T(8,128)(2,1)S(1)}, bf16[512,512]{1,0:T(8,128)(2,1)S(1)}, u32[]{:S(2)}, u32[]{:S(2)}) %collective-permute-start.36) | collective-permute-done | bytes 524320 | tf_op jit(solution)/shard_map/ppermute | solution.py:142
  530.2 11.3 %collective-permute-start.47 = (bf16[128,256]{0,1:T(8,128)(2,1)S(1)}, bf16[128,256]{0,1:T(8,128)(2,1)S(1)}, u32[]{:S(2)}, u32[]{:S(2)}) collective-permute-start(bf16[128,256]{0,1:T(8,128)(2,1)S(1)} %copy.87), channel_id=1, source_target_pairs={{0,1},{1,2},{2,3},{3,0},{4,5},{5,6},{6,7},{7,4},{8,9},{9,10},{10,1... | collective-permute-start | bytes 196616 | tf_op jit(solution)/shard_map/ppermute | solution.py:150
  586.4 19.6 %reduce-scatter.9.cloned.1.call-done = bf16[256,2048]{1,0:T(8,128)(2,1)} async-done(((bf16[1024,2048]{1,0:T(8,128)(2,1)}), bf16[256,2048]{1,0:T(8,128)(2,1)}) %reduce-scatter.9.cloned.1.call-update) | async-done | bytes 1048592 | tf_op jit(solution)/shard_map/reduce_scatter | solution.py:191
  623.9 8.9 %collective-permute-done.49 = bf16[256,512]{1,0:T(8,128)(2,1)S(1)} collective-permute-done((bf16[256,512]{1,0:T(8,128)(2,1)S(1)}, bf16[256,512]{1,0:T(8,128)(2,1)S(1)}, u32[]{:S(2)}, u32[]{:S(2)}) %collective-permute-start.49) | collective-permute-done | bytes 262176 | tf_op jit(solution)/shard_map/ppermute | solution.py:150
  (514 shorter events, 365.7 us)
Async XLA Ops:
  7.2 139.7 %all-gather.12.cloned.1.call-start = ((), (), s32[]{:S(2)}) async-start(), calls=%async_computation.10 | async-start | bytes 1310720 | tf_op jit(solution)/shard_map/all_gather | solution.py:338
  20.6 135.6 %all-gather.6.cloned.1.call-start = ((), (), s32[]{:S(2)}) async-start(), calls=%async_computation.4 | async-start | bytes 1966080 | tf_op jit(solution)/shard_map/all_gather | solution.py:335
  29.3 213.7 %all-gather.8.cloned.1.call-start = ((), (), s32[]{:S(2)}) async-start(), calls=%async_computation.5 | async-start | bytes 5242880 | tf_op jit(solution)/shard_map/all_gather | solution.py:339
  36.6 26.4 %collective-permute-start.22 = (bf16[256,512]{0,1:T(8,128)(2,1)S(1)}, bf16[256,512]{0,1:T(8,128)(2,1)S(1)}, u32[]{:S(2)}, u32[]{:S(2)}) collective-permute-start(bf16[256,512]{0,1:T(8,128)(2,1)S(1)} %maximum_select_fusion.2), channel_id=1, source_target_pairs={{0,2},{1,3},{2,0},{3,1},{4,6},{5,7},{6,4},{7,5},{8,10},{9,11},{10,... | collective-permute-start | bytes 786440 | tf_op jit(solution)/shard_map/ppermute | solution.py:150
  39.7 23.3 %collective-permute-start.21 = (bf16[256,512]{0,1:T(8,128)(2,1)S(1)}, bf16[256,512]{0,1:T(8,128)(2,1)S(1)}, u32[]{:S(2)}, u32[]{:S(2)}) collective-permute-start(bf16[256,512]{0,1:T(8,128)(2,1)S(1)} %maximum_select_fusion.2), channel_id=1, source_target_pairs={{0,1},{1,2},{2,3},{3,0},{4,5},{5,6},{6,7},{7,4},{8,9},{9,10},{10,1... | collective-permute-start | bytes 786440 | tf_op jit(solution)/shard_map/ppermute | solution.py:150
  64.1 189.3 %all-gather.10.cloned.1.call-start = ((), (), s32[]{:S(2)}) async-start(), calls=%async_computation.6 | async-start | bytes 5242880 | tf_op jit(solution)/shard_map/all_gather | solution.py:340
  71.8 77.4 %collective-permute-start = (bf16[512,1024]{1,0:T(8,128)(2,1)}, bf16[512,1024]{1,0:T(8,128)(2,1)}, u32[]{:S(2)}, u32[]{:S(2)}) collective-permute-start(bf16[512,1024]{1,0:T(8,128)(2,1)} %fusion.61), channel_id=1, source_target_pairs={{0,4},{1,5},{6,2},{7,3},{8,12},{9,13},{14,10},{15,11},{16,20},{17,... | collective-permute-start | bytes 3145736 | tf_op jit(solution)/shard_map/ppermute | solution.py:142
  75.9 36.4 %collective-permute-start.24 = (bf16[128,512]{0,1:T(8,128)(2,1)}, bf16[128,512]{0,1:T(8,128)(2,1)S(1)}, u32[]{:S(2)}, u32[]{:S(2)}) collective-permute-start(bf16[128,512]{0,1:T(8,128)(2,1)} %get-tuple-element.236), channel_id=1, source_target_pairs={{0,4},{4,0},{1,5},{5,1},{2,6},{6,2},{3,7},{7,3},{8,12},{12,8},{9,1... | collective-permute-start | bytes 393224 | tf_op jit(solution)/shard_map/ppermute | solution.py:138
  75.9 32.0 %collective-permute-start.4 = (bf16[512,1024]{1,0:T(8,128)(2,1)S(1)}, bf16[512,1024]{1,0:T(8,128)(2,1)}, u32[]{:S(2)}, u32[]{:S(2)}) collective-permute-start(bf16[512,1024]{1,0:T(8,128)(2,1)S(1)} %collective-permute-done.3), channel_id=1, source_target_pairs={{1,0},{6,7},{9,8},{14,15},{17,16},{22,23},{25,24},{30,31}} | collective-permute-start | bytes 3145736 | tf_op jit(solution)/shard_map/ppermute | solution.py:142
  78.6 41.1 %collective-permute-start.7 = (bf16[512,1024]{1,0:T(8,128)(2,1)}, bf16[512,1024]{1,0:T(8,128)(2,1)}, u32[]{:S(2)}, u32[]{:S(2)}) collective-permute-start(bf16[512,1024]{1,0:T(8,128)(2,1)} %collective-permute-done.6), channel_id=1, source_target_pairs={{1,0},{6,7},{9,8},{14,15},{17,16},{22,23},{25,24},{30,31}} | collective-permute-start | bytes 3145736 | tf_op jit(solution)/shard_map/ppermute | solution.py:142
  92.2 57.1 %collective-permute-start.2 = (bf16[512,1024]{1,0:T(8,128)(2,1)}, bf16[512,1024]{1,0:T(8,128)(2,1)}, u32[]{:S(2)}, u32[]{:S(2)}) collective-permute-start(bf16[512,1024]{1,0:T(8,128)(2,1)} %collective-permute-done.1), channel_id=1, source_target_pairs={{0,4},{1,5},{6,2},{7,3},{8,12},{9,13},{14,10},{15,11},{16,20},{17,... | collective-permute-start | bytes 3145736 | tf_op jit(solution)/shard_map/ppermute | solution.py:142
  109.3 40.0 %collective-permute-start.5 = (bf16[512,1024]{1,0:T(8,128)(2,1)S(1)}, bf16[512,1024]{1,0:T(8,128)(2,1)}, u32[]{:S(2)}, u32[]{:S(2)}) collective-permute-start(bf16[512,1024]{1,0:T(8,128)(2,1)S(1)} %broadcast_select_fusion.1), channel_id=1, source_target_pairs={{0,4},{1,5},{6,2},{7,3},{8,12},{9,13},{14,10},{15,11},{16,20},{17,... | collective-permute-start | bytes 3145736 | tf_op jit(solution)/shard_map/ppermute | solution.py:142
  146.4 382.4 %reduce-scatter.13.cloned.1.call-start = ((), (), s32[]{:S(2)}) async-start(), calls=%async_computation.11 | async-start | bytes 1310720
  149.2 64.3 %collective-permute-start.18 = (bf16[4,128,1024]{2,1,0:T(8,128)(2,1)}, bf16[4,128,1024]{2,1,0:T(8,128)(2,1)}, u32[]{:S(2)}, u32[]{:S(2)}) collective-permute-start(bf16[4,128,1024]{2,1,0:T(8,128)(2,1)} %bitcast.182), channel_id=1, source_target_pairs={{0,4},{4,0},{1,5},{5,1},{2,6},{6,2},{3,7},{7,3},{8,12},{12,8},{9,1... | collective-permute-start | bytes 3145736 | tf_op jit(solution)/shard_map/ppermute | solution.py:138
  319.9 110.0 %collective-permute-start.44 = (bf16[4,1,128,1024]{3,2,1,0:T(8,128)(2,1)}, bf16[4,1,128,1024]{3,2,1,0:T(8,128)(2,1)}, u32[]{:S(2)}, u32[]{:S(2)}) collective-permute-start(bf16[4,1,128,1024]{3,2,1,0:T(8,128)(2,1)} %constant_dynamic-slice_fusion.7), channel_id=1, source_target_pairs={{0,4},{4,0},{1,5},{5,1},{2,6},{6,2},{3,7},{7,3},{8,12},{12,8},{9,1... | collective-permute-start | bytes 3145736 | tf_op jit(solution)/shard_map/ppermute | solution.py:138
  432.6 116.2 %reduce-scatter.7.cloned.1.call-start = ((), (), s32[]{:S(2)}) async-start(), calls=%async_computation.7 | async-start | bytes 1966080 | tf_op jit(solution)/shard_map/reduce_scatter | solution.py:396
  447.4 129.5 %reduce-scatter.11.cloned.1.call-start = ((), (), s32[]{:S(2)}) async-start(), calls=%async_computation.9 | async-start | bytes 5242880 | tf_op jit(solution)/shard_map/reduce_scatter | solution.py:191
  457.7 148.3 %reduce-scatter.9.cloned.1.call-start = ((), (), s32[]{:S(2)}) async-start(), calls=%async_computation.8 | async-start | bytes 5242880 | tf_op jit(solution)/shard_map/reduce_scatter | solution.py:191
  485.8 23.5 %collective-permute-start.37 = (bf16[512,512]{1,0:T(8,128)(2,1)S(1)}, bf16[512,512]{1,0:T(8,128)(2,1)S(1)}, u32[]{:S(2)}, u32[]{:S(2)}) collective-permute-start(bf16[512,512]{1,0:T(8,128)(2,1)S(1)} %get-tuple-element.179), channel_id=1, source_target_pairs={{0,1},{3,2},{4,5},{7,6},{8,9},{11,10},{12,13},{15,14},{16,17},{19,... | collective-permute-start | bytes 1572872 | tf_op jit(solution)/shard_map/ppermute | solution.py:142
  487.1 32.9 %collective-permute-start.36 = (bf16[512,512]{1,0:T(8,128)(2,1)S(1)}, bf16[512,512]{1,0:T(8,128)(2,1)S(1)}, u32[]{:S(2)}, u32[]{:S(2)}) collective-permute-start(bf16[512,512]{1,0:T(8,128)(2,1)S(1)} %get-tuple-element.177), channel_id=1, source_target_pairs={{0,1},{1,0},{2,3},{3,2},{4,5},{5,4},{6,7},{7,6},{8,9},{9,8},{10,11... | collective-permute-start | bytes 1572872 | tf_op jit(solution)/shard_map/ppermute | solution.py:142
  528.6 24.5 %collective-permute-start.41 = (bf16[512,512]{1,0:T(8,128)(2,1)S(1)}, bf16[512,512]{1,0:T(8,128)(2,1)S(1)}, u32[]{:S(2)}, u32[]{:S(2)}) collective-permute-start(bf16[512,512]{1,0:T(8,128)(2,1)S(1)} %get-tuple-element.175), channel_id=1, source_target_pairs={{0,4},{4,0},{1,5},{5,1},{2,6},{6,2},{3,7},{7,3},{8,12},{12,8},{9,1... | collective-permute-start | bytes 1572872 | tf_op jit(solution)/shard_map/ppermute | solution.py:138
  578.9 31.6 %collective-permute-start.52 = (bf16[256,512]{1,0:T(8,128)(2,1)}, bf16[256,512]{1,0:T(8,128)(2,1)S(1)}, u32[]{:S(2)}, u32[]{:S(2)}) collective-permute-start(bf16[256,512]{1,0:T(8,128)(2,1)} %get-tuple-element.206), channel_id=1, source_target_pairs={{0,3},{1,0},{2,1},{3,2},{4,7},{5,4},{6,5},{7,6},{8,11},{9,8},{10,9... | collective-permute-start | bytes 786440 | tf_op jit(solution)/shard_map/ppermute | solution.py:150
  580.7 31.0 %collective-permute-start.54 = (bf16[256,512]{1,0:T(8,128)(2,1)}, bf16[256,512]{1,0:T(8,128)(2,1)}, u32[]{:S(2)}, u32[]{:S(2)}) collective-permute-start(bf16[256,512]{1,0:T(8,128)(2,1)} %get-tuple-element.207), channel_id=1, source_target_pairs={{0,1},{1,2},{2,3},{3,0},{4,5},{5,6},{6,7},{7,4},{8,9},{9,10},{10,1... | collective-permute-start | bytes 786440 | tf_op jit(solution)/shard_map/ppermute | solution.py:150
  580.9 30.7 %collective-permute-start.53 = (bf16[256,512]{1,0:T(8,128)(2,1)}, bf16[256,512]{1,0:T(8,128)(2,1)}, u32[]{:S(2)}, u32[]{:S(2)}) collective-permute-start(bf16[256,512]{1,0:T(8,128)(2,1)} %get-tuple-element.208), channel_id=1, source_target_pairs={{0,2},{1,3},{2,0},{3,1},{4,6},{5,7},{6,4},{7,5},{8,10},{9,11},{10,... | collective-permute-start | bytes 786440 | tf_op jit(solution)/shard_map/ppermute | solution.py:150
  (154 other events, 1643.6 us)
Sparse Core Ops, SparseCore 0:
  20.7 25.8 all-gather.11
  49.1 30.8 all-gather.5
  81.8 52.4 all-gather.7
  146.5 50.6 all-gather.9
  432.8 27.2 reduce-scatter.12
  462.9 31.1 reduce-scatter.6
  497.0 52.5 reduce-scatter.10
  552.7 53.2 reduce-scatter.8
